TPU v7x, 8 devices: a whole 2x2x1 slice. The times are simulated.
8 devices in a mesh: rep: 1 (over z), kv: 8 (over y, x, core).
Axes of the slice: x: 2, y: 2, z: 1, core: 2. Of those that a mesh axis runs over, the one named last changes fastest.
Arguments:
- embeds: bfloat16 [2, 512, 4096], P(None, ('rep', 'kv'))
- w_query: bfloat16 [2, 4096, 4096], replicated
- w_key: bfloat16 [2, 4096, 1024], replicated
- w_value: bfloat16 [2, 4096, 1024], replicated
- w_out: bfloat16 [2, 4096, 4096], replicated
- w_up: bfloat16 [2, 4096, 14336], replicated
- w_down: bfloat16 [2, 14336, 4096], replicated
- k_pool: bfloat16 [1536, 2, 16, 8, 128], P(('rep', 'kv'))
- v_pool: bfloat16 [1536, 2, 16, 8, 128], P(('rep', 'kv'))
- new_table: int32 [512, 2], P('rep')
- seq_lens: int32 [512], P('rep')
- mig_src: int32 [64], P('rep')
- mig_dst: int32 [64], P('rep')
Outputs:
- output 1: bfloat16 [2, 512, 4096], P(None, ('rep', 'kv'))
- output 2: bfloat16 [1536, 2, 16, 8, 128], P(('rep', 'kv'))
- output 3: bfloat16 [1536, 2, 16, 8, 128], P(('rep', 'kv'))
All inputs are finite; a program needn't handle non-finite values.
Results may differ from a plain program's by a relative error of at most 0.0168677.
Values are sent between devices in bfloat16 or wider.
A program may use at most 2.75 GiB of HBM per device.

v0:
```python
import functools

import jax
import jax.numpy as jnp
from jax import lax
from jax.experimental import pallas as pl
from jax.experimental.pallas import tpu as pltpu
from jax.sharding import PartitionSpec as P


STEPS = 2
I32 = jnp.int32


def excl_cumsum(values):
    n = values.shape[0]
    before = jnp.arange(n)[None, :] < jnp.arange(n)[:, None]
    return jnp.sum(jnp.where(before, values[None, :], 0), axis=1)


def masked_pick(mask, values):
    return jnp.sum(jnp.where(mask, values, 0), axis=-1)


def place_sequences(pref, group_size, per_dev):
    count = pref.shape[0]
    ids = jnp.arange(count)
    earlier = ids[None, :] < ids[:, None]
    rank = jnp.sum((pref[None, :] == pref[:, None]) & earlier, axis=1)
    wanted = jnp.sum(pref[None, :] == jnp.arange(group_size)[:, None], axis=1)
    free = jnp.maximum(per_dev - wanted, 0)
    free_end = excl_cumsum(free) + free
    over = rank >= per_dev
    over_rank = jnp.sum(over[None, :] & earlier, axis=1)
    spill = jnp.sum(over_rank[:, None] >= free_end[None, :], axis=1)
    dev = jnp.where(over, spill, pref)
    pos = jnp.sum((dev[None, :] == dev[:, None]) & earlier, axis=1)
    return dev.astype(I32), pos.astype(I32)


def any_spec():
    return pl.BlockSpec(memory_space=pl.ANY)


def smem_spec():
    return pl.BlockSpec(memory_space=pltpu.SMEM)


def vmem_spec():
    return pl.BlockSpec(memory_space=pltpu.VMEM)


def start(copy):
    copy.start()


def wait(copy):
    copy.wait()


def for_all(count, table, row, make, act):
    def body(e, carry):
        @pl.when(table[row, e] >= 0)
        def _():
            for copy in make(e):
                act(copy)

        return carry

    lax.fori_loop(0, count, body, 0)


def page_copies(layer, k_pool, v_pool, slot, k_dst, v_dst, sem):
    return (pltpu.make_async_copy(k_pool.at[slot, layer], k_dst, sem), pltpu.make_async_copy(v_pool.at[slot, layer], v_dst, sem))


def pack_pages_kernel(layers, meta, k_pool, v_pool, *rest):
    outs = rest[:len(layers)]
    stage, in_sem, out_sem = rest[-3:]
    page_len = k_pool.shape[2]
    count = stage.shape[2] // page_len

    def fetch(at):
        def make(e):
            part = pl.ds(e * page_len, page_len)
            return page_copies(layers[at], k_pool, v_pool, meta[0, e], stage.at[at, 0, part], stage.at[at, 1, part], in_sem.at[at])

        return make

    for at in range(len(layers)):
        for_all(count, meta, 0, fetch(at), start)

    def wipe(e, carry):
        @pl.when(meta[0, e] < 0)
        def _():
            for at in range(len(layers)):
                for which in range(2):
                    stage[at, which, pl.ds(e * page_len, page_len)] = jnp.zeros((page_len,) + stage.shape[3:], stage.dtype)

        return carry

    lax.fori_loop(0, count, wipe, 0)
    for at in range(len(layers)):
        for_all(count, meta, 0, fetch(at), wait)
        pltpu.make_async_copy(stage.at[at], outs[at], out_sem.at[at]).start()
    for at in range(len(layers)):
        pltpu.make_async_copy(stage.at[at], outs[at], out_sem.at[at]).wait()


def pack_pages(layers, k_pool, v_pool, slot_of):
    shape = (2, slot_of.shape[0] * k_pool.shape[2]) + k_pool.shape[3:]
    return pl.pallas_call(
        functools.partial(pack_pages_kernel, layers),
        out_shape=[jax.ShapeDtypeStruct(shape, k_pool.dtype)] * len(layers),
        in_specs=[smem_spec(), any_spec(), any_spec()],
        out_specs=[any_spec()] * len(layers),
        scratch_shapes=[pltpu.VMEM((len(layers),) + shape, k_pool.dtype), pltpu.SemaphoreType.DMA((len(layers),)), pltpu.SemaphoreType.DMA((len(layers),))],
    )(slot_of[None, :].astype(I32), k_pool, v_pool)


def pack_rows_kernel(layers, meta, k_pool, v_pool, *rest):
    outs = rest[:len(layers)]
    pages, stage, in_sem, out_sem = rest[-4:]
    count = pages.shape[1]
    page_len = k_pool.shape[2]

    def fetch(at):
        return lambda e: page_copies(layers[at], k_pool, v_pool, meta[0, e], pages.at[at, e, 0], pages.at[at, e, 1], in_sem.at[at])

    for at in range(len(layers)):
        for_all(count, meta, 0, fetch(at), start)
    nothing = jnp.zeros((page_len,) + stage.shape[3:], stage.dtype)

    def wipe(i, carry):
        for at in range(len(layers)):
            for which in range(2):
                stage[at, which, pl.ds(i * page_len, page_len)] = nothing
        return carry

    lax.fori_loop(0, stage.shape[2] // page_len, wipe, 0)
    for at in range(len(layers)):
        for_all(count, meta, 0, fetch(at), wait)

        def place(e, carry):
            @pl.when(meta[0, e] >= 0)
            def _():
                for which in range(2):
                    stage[at, which, pl.ds(meta[1, e], page_len)] = pages[at, e, which]
                    stage[at, which, pl.ds(meta[1, e] + meta[2, e], page_len)] = nothing

            return carry

        lax.fori_loop(0, count, place, 0)
        pltpu.make_async_copy(stage.at[at], outs[at], out_sem.at[at]).start()
    for at in range(len(layers)):
        pltpu.make_async_copy(stage.at[at], outs[at], out_sem.at[at]).wait()


def pack_rows(layers, k_pool, v_pool, meta, cap, spare=()):
    count = meta.shape[1]
    page_len = k_pool.shape[2]
    shape = (2, cap + 2 * page_len) + k_pool.shape[3:]
    outs = [jax.ShapeDtypeStruct(shape, k_pool.dtype)] * len(layers) + [jax.ShapeDtypeStruct(s, k_pool.dtype) for s in spare]
    return pl.pallas_call(
        functools.partial(pack_rows_kernel, layers),
        out_shape=outs,
        in_specs=[smem_spec(), any_spec(), any_spec()],
        out_specs=[any_spec()] * len(outs),
        scratch_shapes=[
            pltpu.VMEM((len(layers), count, 2) + k_pool.shape[2:], k_pool.dtype),
            pltpu.VMEM((len(layers),) + shape, k_pool.dtype),
            pltpu.SemaphoreType.DMA((len(layers),)),
            pltpu.SemaphoreType.DMA((len(layers),)),
        ],
    )(meta.astype(I32), k_pool, v_pool)


LOCAL, MOVED, NEXT, OTHER = range(4)
MOVED_ROWS = 10
NEAR_ROWS = 9


def attend_kernel(layer, seqs, page_len, q_per_kv, unroll, meta, q_ref, new_ref, k_pool, v_pool, moved, near, other, out_ref, k_buf, v_buf, k_sem, v_sem):
    kv_heads, head_dim = k_buf.shape[2:]

    def launch(j, carry):
        for page in range(2):
            kind = meta[2 * page, j]
            index = meta[2 * page + 1, j]

            def both(k_src, v_src):
                dst = pl.ds(page * page_len, page_len)
                pltpu.make_async_copy(k_src, k_buf.at[j, dst], k_sem.at[j]).start()
                pltpu.make_async_copy(v_src, v_buf.at[j, dst], v_sem.at[j]).start()

            @pl.when(kind == LOCAL)
            def _():
                both(k_pool.at[index, layer], v_pool.at[index, layer])

            @pl.when(kind > LOCAL)
            def _():
                part = pl.ds(index, page_len)

                @pl.when(kind == MOVED)
                def _():
                    both(moved.at[0, part], moved.at[1, part])

                @pl.when(kind == NEXT)
                def _():
                    both(near.at[0, part], near.at[1, part])

                @pl.when(kind == OTHER)
                def _():
                    both(other.at[index, 0, layer], other.at[index, 1, layer])
        return carry

    lax.fori_loop(0, seqs, launch, 0)

    rows = STEPS * kv_heads * q_per_kv
    cols = 2 * page_len * kv_heads
    row_id = lax.broadcasted_iota(I32, (rows, cols), 0)
    col_id = lax.broadcasted_iota(I32, (rows, cols), 1)
    row_step = row_id // (kv_heads * q_per_kv)
    own_head = (col_id % kv_heads) == (row_id % (kv_heads * q_per_kv)) // q_per_kv
    lag = jnp.where(own_head, col_id // kv_heads - row_step, 1 << 20)

    def body(i, carry):
        for u in range(unroll):
            j = i * unroll + u
            pltpu.make_async_copy(k_buf.at[j], k_buf.at[j], k_sem.at[j]).wait()
            pltpu.make_async_copy(v_buf.at[j], v_buf.at[j], v_sem.at[j]).wait()
        for u in range(unroll):
            j = i * unroll + u
            length = meta[4, j]
            for step in range(STEPS):
                k_buf[j, length + step] = new_ref[j, 0, step]
                v_buf[j, length + step] = new_ref[j, 1, step]
        for u in range(unroll):
            j = i * unroll + u
            length = meta[4, j]
            keys = k_buf[j].reshape(cols, head_dim)
            vals = v_buf[j].reshape(cols, head_dim)
            query = q_ref[j].reshape(rows, head_dim)
            scores = lax.dot_general(query, keys, (((1,), (1,)), ((), ())), preferred_element_type=jnp.float32)
            scores = jnp.where(lag <= length, scores * head_dim ** -0.5, -jnp.inf)
            top = jnp.max(scores, axis=1, keepdims=True)
            probs = jnp.exp(scores - top)
            total = jnp.sum(probs, axis=1, keepdims=True)
            out = jnp.dot(probs.astype(vals.dtype), vals, preferred_element_type=jnp.float32) / total
            out_ref[j] = out.astype(out_ref.dtype).reshape(out_ref.shape[1:])
        return carry

    lax.fori_loop(0, seqs // unroll, body, 0)


def attend(layer, queries, new_rows, k_pool, v_pool, moved, near, other, meta):
    seqs = queries.shape[0]
    page_len, kv_heads, head_dim = k_pool.shape[2:]
    num_heads = queries.shape[2]
    buf = pltpu.VMEM((seqs, 2 * page_len, kv_heads, head_dim), k_pool.dtype)
    return pl.pallas_call(
        functools.partial(attend_kernel, layer, seqs, page_len, num_heads // kv_heads, 4),
        out_shape=jax.ShapeDtypeStruct(queries.shape, queries.dtype),
        in_specs=[smem_spec(), vmem_spec(), vmem_spec()] + [any_spec()] * 5,
        out_specs=vmem_spec(),
        scratch_shapes=[buf, buf, pltpu.SemaphoreType.DMA((seqs,)), pltpu.SemaphoreType.DMA((seqs,))],
        cost_estimate=pl.CostEstimate(flops=10 ** 10, bytes_accessed=10 ** 7, transcendentals=10 ** 6),
    )(meta, queries, new_rows, k_pool, v_pool, moved, near, other)


COPY_SLOTS = 16


def copy_kernel(k_pool, v_pool, k_out, v_out, stage, in_sem, out_sem):
    chunks = k_pool.shape[0] // COPY_SLOTS
    for pool, which in ((k_pool, 0), (v_pool, 1)):
        for c in range(chunks):
            part = pl.ds(c * COPY_SLOTS, COPY_SLOTS)
            pltpu.make_async_copy(pool.at[part], stage.at[which, part], in_sem.at[which, c]).start()
    for pool, out, which in ((k_pool, k_out, 0), (v_pool, v_out, 1)):
        for c in range(chunks):
            part = pl.ds(c * COPY_SLOTS, COPY_SLOTS)
            pltpu.make_async_copy(pool.at[part], stage.at[which, part], in_sem.at[which, c]).wait()
            pltpu.make_async_copy(stage.at[which, part], out.at[part], out_sem.at[which, c]).start()
    for out, which in ((k_out, 0), (v_out, 1)):
        for c in range(chunks):
            part = pl.ds(c * COPY_SLOTS, COPY_SLOTS)
            pltpu.make_async_copy(stage.at[which, part], out.at[part], out_sem.at[which, c]).wait()


def copy_pools(k_pool, v_pool):
    chunks = k_pool.shape[0] // COPY_SLOTS
    pool = jax.ShapeDtypeStruct(k_pool.shape, k_pool.dtype)
    return pl.pallas_call(
        copy_kernel,
        out_shape=[pool, pool],
        in_specs=[any_spec(), any_spec()],
        out_specs=[any_spec(), any_spec()],
        scratch_shapes=[pltpu.VMEM((2,) + k_pool.shape, k_pool.dtype), pltpu.SemaphoreType.DMA((2, chunks)), pltpu.SemaphoreType.DMA((2, chunks))],
        name='copy_pools',
    )(k_pool, v_pool)


def finish_kernel(layers, slots, entries, mig, owner, k_in, v_in, *rest):
    del k_in, v_in
    moved, own, prev, far = (rest[i * layers:(i + 1) * layers] for i in range(4))
    k_out, v_out, zeros, stage, row_stage, far_stage, zero_sem, in_sem, out_sem, row_in_sem, row_sem, far_sem = rest[4 * layers:]
    page_len = k_out.shape[2]
    seats = own[0].shape[0]

    def fetch(e):
        part = pl.ds(e * page_len, page_len)
        return [pltpu.make_async_copy(moved[layer].at[which, part], stage.at[e, layer, which], in_sem.at[e]) for layer in range(layers) for which in range(2)]

    def put(e):
        return [pltpu.make_async_copy(stage.at[e, layer, which], out.at[mig[1, e], layer], out_sem.at[0]) for layer in range(layers) for which, out in enumerate((k_out, v_out))]

    def clear(e):
        return [pltpu.make_async_copy(zeros, out.at[mig[0, e]], zero_sem.at[0]) for out in (k_out, v_out)]

    def load(layer):
        return (pltpu.make_async_copy(own[layer], row_stage.at[layer, pl.ds(0, seats)], row_in_sem.at[layer]),
                pltpu.make_async_copy(prev[layer], row_stage.at[layer, pl.ds(seats, seats)], row_in_sem.at[layer]))

    def fill(j):
        dst = pl.ds(owner[1, j], STEPS)
        return [pltpu.make_async_copy(row_stage.at[layer, owner[0, j], which], out.at[j, layer, dst], row_sem.at[0]) for layer in range(layers) for which, out in enumerate((k_out, v_out))]

    for_all(entries, mig, 1, fetch, start)
    for layer in range(layers):
        for copy in load(layer):
            copy.start()
    zeros[...] = jnp.zeros_like(zeros)

    def relay(e, carry):
        @pl.when(mig[1, e] >= 0)
        def _():
            for copy in fetch(e):
                copy.wait()
            for copy in put(e):
                copy.start()

        return carry

    lax.fori_loop(0, entries, relay, 0)
    for_all(entries, mig, 0, clear, start)
    for_all(entries, mig, 1, put, wait)
    for layer in range(layers):
        for copy in load(layer):
            copy.wait()
    for_all(slots, owner, 0, fill, start)

    def from_far(j, carry):
        @pl.when(owner[2, j] >= 0)
        def _():
            dst = pl.ds(owner[1, j], STEPS)
            for layer in range(layers):
                copy = pltpu.make_async_copy(far[layer].at[owner[2, j]], far_stage, far_sem.at[0])
                copy.start()
                copy.wait()
                for which, out in enumerate((k_out, v_out)):
                    copy = pltpu.make_async_copy(far_stage.at[which], out.at[j, layer, dst], far_sem.at[0])
                    copy.start()
                    copy.wait()

        return carry

    lax.fori_loop(0, slots, from_far, 0)
    for_all(entries, mig, 0, clear, wait)
    for_all(slots, owner, 0, fill, wait)


def finish_pools(k_pool, v_pool, moved, own, prev, far, mig, owner):
    slots, layers = k_pool.shape[:2]
    entries = mig.shape[1]
    pool = jax.ShapeDtypeStruct(k_pool.shape, k_pool.dtype)
    row_shape = own[0].shape
    return pl.pallas_call(
        functools.partial(finish_kernel, layers, slots, entries),
        out_shape=[pool, pool],
        in_specs=[smem_spec(), smem_spec()] + [any_spec()] * (2 + 4 * layers),
        out_specs=[any_spec(), any_spec()],
        input_output_aliases={2: 0, 3: 1},
        scratch_shapes=[
            pltpu.VMEM(k_pool.shape[1:], k_pool.dtype),
            pltpu.VMEM((entries, layers, 2) + k_pool.shape[2:], k_pool.dtype),
            pltpu.VMEM((layers, 2 * row_shape[0]) + row_shape[1:], k_pool.dtype),
            pltpu.VMEM(row_shape[1:], k_pool.dtype),
            pltpu.SemaphoreType.DMA((1,)),
            pltpu.SemaphoreType.DMA((entries,)),
            pltpu.SemaphoreType.DMA((1,)),
            pltpu.SemaphoreType.DMA((layers,)),
            pltpu.SemaphoreType.DMA((1,)),
            pltpu.SemaphoreType.DMA((1,)),
        ],
        name='finish_pools',
    )(mig, owner, k_pool, v_pool, *moved, *own, *prev, *far)


def dense(hidden, weight):
    return jnp.dot(hidden, weight, preferred_element_type=jnp.float32)


def pair_mlp(hidden, w_up, w_down, layer, core, pairs):
    rows = hidden.shape[0]
    width, full = w_up.shape[1:]
    half = full // 2
    both = jnp.concatenate([hidden, lax.ppermute(hidden, 'kv', pairs)])
    up_proj = dense(both, lax.dynamic_slice(w_up, (layer, 0, core * half), (1, width, half))[0]).astype(jnp.bfloat16)
    act = jax.nn.gelu(up_proj.astype(jnp.float32), approximate=True).astype(jnp.bfloat16)
    part = dense(act, lax.dynamic_slice(w_down, (layer, core * half, 0), (1, half, width))[0])
    rest = lax.ppermute(part[rows:], 'kv', pairs)
    return (hidden.astype(jnp.float32) + (part[:rows] + rest)).astype(jnp.bfloat16)


def shift_by(count, distance):
    return [(i, (i + distance) % count) for i in range(count)]


ROUND_PAGES = 8


def other_pages(k_pool, v_pool, buffer, src, slot, dst, target, wanted, me, group_size):
    entry_ids = jnp.arange(src.shape[0])
    rank = masked_pick((src[None, :] == src[:, None]) & wanted[None, :] & (entry_ids[None, :] < entry_ids[:, None]), 1)
    most = jnp.max(jnp.where(wanted, rank + 1, 0))
    seat = jnp.where(wanted, src * src.shape[0] + rank, -1)

    def body(carry):
        done, buf = carry
        seats = ((jnp.arange(group_size) * src.shape[0])[:, None] + done + jnp.arange(ROUND_PAGES)[None, :]).reshape(-1)
        hit = seat[None, :] == seats[:, None]
        seat_slot = masked_pick(hit, slot[None, :])
        seat_target = jnp.where(jnp.any(hit & (dst == me)[None, :], axis=1), masked_pick(hit, target[None, :]), buf.shape[0])
        my_slots = lax.dynamic_slice_in_dim(seat_slot, me * ROUND_PAGES, ROUND_PAGES)
        pages = jnp.stack([jnp.take(k_pool, my_slots, axis=0), jnp.take(v_pool, my_slots, axis=0)], axis=1)
        gathered = lax.all_gather(pages, 'kv', axis=0, tiled=True)
        return done + ROUND_PAGES, buf.at[seat_target].set(gathered, mode='drop')

    return lax.while_loop(lambda carry: carry[0] < most, body, (jnp.zeros((), I32), buffer))[1]


def solution(mesh):
    group_size = mesh.shape['kv']
    pool_spec = P(('rep', 'kv'))
    tok_spec = P(None, ('rep', 'kv'), None)

    def device_fn(embeds, w_query, w_key, w_value, w_out, w_up, w_down, k_pool, v_pool, new_table, seq_lens, mig_src, mig_dst):
        me = lax.axis_index('kv')
        slots, layers, page_len, kv_heads, head_dim = k_pool.shape
        per_dev, width = embeds.shape[1:]
        seq_count, page_count = new_table.shape
        num_heads = w_query.shape[2] // head_dim
        pairs = [(i, i ^ 1) for i in range(group_size)]

        remap = new_table[:, :, None] == mig_dst
        is_moved = jnp.any(remap, axis=-1)
        old_table = jnp.where(is_moved, masked_pick(remap, mig_src), new_table)
        page_src = old_table // slots
        page_slot = old_table % slots
        dev, pos = place_sequences(page_src[:, 0], group_size, per_dev)
        place = dev * per_dev + pos

        page_ids = jnp.arange(page_count, dtype=I32)[None, :]
        page_rows = jnp.where(page_ids == 0, page_len, seq_lens[:, None] - page_len)

        src_dev, dst_dev = mig_src // slots, mig_dst // slots
        clear_slot = jnp.where(src_dev == me, mig_src % slots, -1)
        fill_slot = jnp.where(dst_dev == me, mig_dst % slots, -1)
        mig_meta = jnp.stack([clear_slot, fill_slot]).astype(I32)
        moved_cap = mig_src.shape[0] * MOVED_ROWS
        moved_rows = jnp.sum(jnp.where(remap, page_rows[:, :, None], 0), axis=(0, 1))
        moved_first = excl_cumsum(moved_rows)
        moved_fits = moved_first + moved_rows <= moved_cap
        moved_meta = jnp.stack([jnp.where(moved_fits, clear_slot, -1), moved_first, moved_rows])
        moved = [lax.psum(pack_rows((0,), k_pool, v_pool, moved_meta, moved_cap)[0], 'kv')]

        is_local = page_src == dev[:, None]
        in_moved = jnp.any(remap & moved_fits, axis=-1) & ~is_local
        same_dev_earlier = (dev[None, :] == dev[:, None]) & (pos[None, :] < pos[:, None])
        near_cap = per_dev * NEAR_ROWS
        by_next = (page_src[:, 1] == (dev + 1) % group_size) & ~is_moved[:, 1]
        near_first = masked_pick(same_dev_earlier & by_next[None, :], page_rows[None, :, 1])
        by_next = by_next & (near_first + page_rows[:, 1] <= near_cap)
        is_near = (page_ids == 1) & by_next[:, None]

        prev = (me + group_size - 1) % group_size
        prev_seat = prev * per_dev + jnp.arange(per_dev, dtype=I32)
        from_here = (place[None, :] == prev_seat[:, None]) & by_next[None, :]
        near_facts = jnp.stack([page_slot[:, 1] + 1, near_first, page_rows[:, 1]])
        near_meta = masked_pick(from_here[None, :, :], near_facts[:, None, :]) - jnp.array([[1], [0], [0]])
        other_shape = (per_dev * page_count, 2) + k_pool.shape[1:]
        far_shape = (seq_count, 2, STEPS, kv_heads, head_dim)
        *near_out, other, far_0, far_1 = pack_rows(tuple(range(layers)), k_pool, v_pool, near_meta, near_cap, [other_shape, far_shape, far_shape])

        my_dev = lax.dynamic_slice_in_dim(dev, me * per_dev, per_dev)
        my_pos = lax.dynamic_slice_in_dim(pos, me * per_dev, per_dev)
        home = jnp.arange(seq_count, dtype=I32) // per_dev
        distance = (dev - home) % group_size
        my_distance = (my_dev - me) % group_size
        at_pos = my_pos[None, :] == jnp.arange(per_dev, dtype=I32)[:, None]

        def send_embeds(step_away, hidden):
            sel = (at_pos & (my_distance == step_away)[None, :]).astype(embeds.dtype)
            rows = jnp.einsum('pb,tbd->ptd', sel, embeds, preferred_element_type=jnp.float32).astype(embeds.dtype)
            if step_away:
                rows = lax.ppermute(rows, 'kv', shift_by(group_size, step_away))
            return hidden + rows

        hidden = jnp.zeros((per_dev, STEPS, width), embeds.dtype)
        for step_away in range(group_size):
            hidden = lax.cond(jnp.any(distance == step_away), functools.partial(send_embeds, step_away), lambda same: same, hidden)
        hidden = hidden.reshape(per_dev * STEPS, width)
        near_out[0], hidden = lax.optimization_barrier((near_out[0], hidden))
        near = [lax.ppermute(near_out[0], 'kv', shift_by(group_size, -1))]

        wanted = ~(is_local | in_moved | is_near)
        kind = jnp.where(is_local, LOCAL, jnp.where(in_moved, MOVED, jnp.where(is_near, NEXT, OTHER)))
        target = pos[:, None] * page_count + page_ids
        entry_dst = jnp.broadcast_to(dev[:, None], page_src.shape)
        other = other_pages(k_pool, v_pool, other, page_src.reshape(-1), page_slot.reshape(-1), entry_dst.reshape(-1), target.reshape(-1), wanted.reshape(-1), me, group_size)
        mine = place[None, :] == (me * per_dev + jnp.arange(per_dev, dtype=I32))[:, None]
        facts = []
        for layer in range(layers):
            moved_at = masked_pick(remap, moved_first) if layer == 0 else masked_pick(remap, jnp.arange(mig_src.shape[0], dtype=I32)) * page_len
            index = jnp.where(is_local, page_slot, jnp.where(in_moved, moved_at, jnp.where(is_near, near_first[:, None], target)))
            facts.append(jnp.stack([kind[:, 0], index[:, 0], kind[:, 1], index[:, 1], seq_lens]))
        attend_meta = masked_pick(mine[None, None, :, :], jnp.stack(facts)[:, :, None, :]).astype(I32)

        row_dst = new_table[:, 1] // slots
        is_far = (row_dst != dev) & (row_dst != (dev + 1) % group_size)
        writes = new_table[None, :, 1] == (me * slots + jnp.arange(slots, dtype=I32))[:, None]
        owner_facts = jnp.stack([jnp.where(is_far, 0, 1 + pos + jnp.where(row_dst == dev, 0, per_dev)), seq_lens - page_len, jnp.where(is_far, 1 + place, 0)])
        owner_meta = (masked_pick(writes[None, :, :], owner_facts[:, None, :]) - jnp.array([[1], [0], [1]])).astype(I32)

        own_rows, prev_rows = [], []
        for layer in range(layers):
            queries = dense(hidden, w_query[layer]).astype(jnp.bfloat16)
            new_keys = dense(hidden, w_key[layer]).astype(jnp.bfloat16)
            new_vals = dense(hidden, w_value[layer]).astype(jnp.bfloat16)
            rows = jnp.stack([new_keys, new_vals]).reshape(2, per_dev, STEPS, kv_heads, head_dim).transpose(1, 0, 2, 3, 4)
            own_rows.append(rows)
            prev_rows.append(lax.ppermute(rows, 'kv', shift_by(group_size, 1)))
            q_rows = queries.reshape(per_dev, STEPS, num_heads, head_dim)
            if layer == 0:
                k_src, v_src, q_rows = lax.optimization_barrier((k_pool, v_pool, q_rows))
                k_base, v_base = copy_pools(k_src, v_src)
                q_rows, k_base, v_base = lax.optimization_barrier((q_rows, k_base, v_base))
            if layer == 0:
                full_out = list(pack_pages(tuple(range(layers)), k_pool, v_pool, clear_slot))
                for after in range(layers - 1, -1, -1):
                    full_out[after], moved[-1] = lax.optimization_barrier((full_out[after], moved[-1]))
                    moved.append(lax.psum(full_out[after], 'kv'))
                moved = [moved[0]] + moved[:0:-1]
            if layer + 1 < layers:
                near_next, near[layer] = lax.optimization_barrier((near_out[layer + 1], near[layer]))
                near.append(lax.ppermute(near_next, 'kv', shift_by(group_size, -1)))
            attn = attend(layer, q_rows, rows, k_pool, v_pool, moved[layer if layer == 0 else layer + 1], near[layer], other, attend_meta[layer]).reshape(per_dev * STEPS, num_heads * head_dim)
            hidden = (hidden.astype(jnp.float32) + dense(attn, w_out[layer])).astype(jnp.bfloat16)
            hidden = pair_mlp(hidden, w_up, w_down, layer, me % 2, pairs)

        far_rows = [lax.cond(jnp.any(is_far), lambda own, far: lax.all_gather(own, 'kv', axis=0, tiled=True), lambda own, far: far, own, far) for own, far in zip(own_rows, (far_0, far_1))]
        k_out, v_out = finish_pools(k_base, v_base, moved[1:], own_rows, prev_rows, far_rows, mig_meta, owner_meta)

        hidden = hidden.reshape(per_dev, STEPS, width)

        def bring_home(step_away, total):
            rows = lax.ppermute(hidden, 'kv', shift_by(group_size, -step_away)) if step_away else hidden
            sel = (at_pos & (my_distance == step_away)[None, :]).astype(hidden.dtype)
            return total + jnp.einsum('pb,ptd->tbd', sel, rows, preferred_element_type=jnp.float32).astype(hidden.dtype)

        y_out = jnp.zeros((STEPS, per_dev, width), hidden.dtype)
        for step_away in range(group_size):
            y_out = lax.cond(jnp.any(distance == step_away), functools.partial(bring_home, step_away), lambda same: same, y_out)
        return y_out, k_out, v_out

    return jax.shard_map(device_fn, mesh=mesh, in_specs=(tok_spec, P(), P(), P(), P(), P(), P(), pool_spec, pool_spec, P('rep', None), P('rep'), P('rep'), P('rep')), out_specs=(tok_spec, pool_spec, pool_spec), check_vma=False)
```

profile of v0, /device:TPU:0, one launch (start us, length us, event | category | flops | bytes accessed | tf_op | source)
XLA Modules:
  0.0 446.0 jit_solution(11757321171493743737)
XLA Ops:
  10.8 6.2 %shard_map.168 = bf16[2,672,8,128]{3,2,1,0:T(8,128)(2,1)} custom-call(s32[3,64]{1,0:T(4,128)} %pad_add_fusion.3.meta, bf16[192,2,16,8,128]{4,3,2,1,0:T(8,128)(2,1)} %k_pool.10, bf16[192,2,16,8,128]{4,3,2,1,0:T(8,128)(2,1)} %v_pool.10), custom_call_target="tpu_custom_call" | custom-call | tf_op jit(solution)/shard_map/pallas_call | solution.py:164
  24.9 25.8 %conditional.19 = (bf16[64,2,4096]{2,0,1:T(8,128)(2,1)S(1)}) conditional(s32[]{:T(128)} %convert_element_type.209, bf16[64,2,4096]{2,0,1:T(8,128)(2,1)S(1)} %get-tuple-element.1075, (s32[64]{0:T(128)S(1)}, pred[64,64]{0,1:T(32,128)(4,1)S(1)}, bf16[2,64,4096]{2,1,0:T(8,128)(2,1)S(1)}, bf16[64,2,4096]{2,0,1:T(8,128)(2,1)S(1)}) %tuple.370), branch_computations={%region_20.21_spmd, %region_21.22_spmd} | conditional | flops 68161600 | bytes 9449904 | solution.py:512
  25.5 24.8 %collective-permute-done = bf16[64,2,4096]{2,0,1:T(8,128)(2,1)S(1)} collective-permute-done((bf16[64,2,4096]{2,0,1:T(8,128)(2,1)S(1)}, bf16[64,2,4096]{2,0,1:T(8,128)(2,1)S(1)}, u32[]{:S(2)}, u32[]{:S(2)}) %collective-permute-start) | collective-permute-done | bytes 1048608 | tf_op jit(solution)/shard_map/cond/branch_1_fun/ppermute | solution.py:507
  55.0 9.3 %shard_map.166 = (bf16[2,608,8,128]{3,2,1,0:T(8,128)(2,1)}, bf16[2,608,8,128]{3,2,1,0:T(8,128)(2,1)}, bf16[128,2,2,16,8,128]{5,4,3,2,1,0:T(8,128)(2,1)}, bf16[51...) custom-call(s32[3,64]{1,0:T(4,128)} %broadcast_add_fusion.2.meta, bf16[192,2,16,8,128]{4,3,2,1,0:T(8,128)(2,1)} %k_pool.10, ...), custom_call_target="tpu_custom_call" | custom-call | tf_op jit(solution)/shard_map/pallas_call | solution.py:164
  64.4 13.5 %fusion.178 = bf16[16,8,32,128]{3,1,2,0:T(8,128)(2,1)S(1)} fusion(bf16[128,4096]{1,0:T(8,128)(2,1)S(1)} %reshape.636, bf16[2,4096,4096]{2,1,0:T(8,128)(2,1)} %param.56), kind=kOutput, calls=%fused_computation.206 | convolution fusion | flops 4295491584 | bytes 35651584 | tf_op jit(solution)/shard_map/dot_general | solution.py:401
  77.9 4.7 %fusion.199 = bf16[16,8,8,128]{3,1,2,0:T(8,128)(2,1)S(1)} fusion(bf16[128,4096]{1,0:T(8,128)(2,1)S(1)} %reshape.636, bf16[2,4096,1024]{2,1,0:T(8,128)(2,1)} %param.58), kind=kOutput, calls=%fused_computation.217 | convolution fusion | flops 1073872896 | bytes 9699328 | tf_op jit(solution)/shard_map/dot_general | solution.py:401
  89.4 7.1 %shard_map.167 = (bf16[2,1024,8,128]{3,2,1,0:T(8,128)(2,1)}, bf16[2,1024,8,128]{3,2,1,0:T(8,128)(2,1)}) custom-call(s32[1,64]{1,0:T(1,128)} %bitcast.338, bf16[192,2,16,8,128]{4,3,2,1,0:T(8,128)(2,1)} %k_pool.10, bf16[192,2,16,8,128]{4,3,2,1,0:T(8,128)(2,1)} %v_pool.10), custom_call_target="tpu_custom_call" | custom-call | tf_op jit(solution)/shard_map/pallas_call | solution.py:112
  97.8 17.5 %copy_pools.1 = (bf16[192,2,16,8,128]{4,3,2,1,0:T(8,128)(2,1)}, bf16[192,2,16,8,128]{4,3,2,1,0:T(8,128)(2,1)}) custom-call(bf16[192,2,16,8,128]{4,3,2,1,0:T(8,128)(2,1)} %k_pool.10, bf16[192,2,16,8,128]{4,3,2,1,0:T(8,128)(2,1)} %v_pool.10), custom_call_target="tpu_custom_call" | custom-call | tf_op jit(solution)/shard_map/copy_pools/pallas_call | solution.py:294
  118.2 22.9 %shard_map.169 = bf16[64,2,32,128]{3,2,1,0:T(8,128)(2,1)} custom-call(s32[5,64]{1,0:T(8,128)} %get-tuple-element.873.meta, bf16[64,2,32,128]{3,2,1,0:T(8,128)(2,1)} %bitcast.307, bf16[64,2,2,8,128]{4,3,2,1,0:T(8,128)(2,1)S(1)} %maximum_bitcast_fusion.new_ref.rest_2_, bf16[192,2,16,8,128]{4,3,2,1,0:T(8,128)(2,1)} %get-tuple-element.1098, ...), custom_call_target="tpu_custom_call" | custom-call | flops 10000000000 | bytes 10000000 | tf_op jit(solution)/shard_map/pallas_call | solution.py:261
  141.1 13.5 %fusion.141 = bf16[128,4096]{1,0:T(8,128)(2,1)S(1)} fusion(bf16[2,4096,4096]{2,1,0:T(8,128)(2,1)} %param.59, bf16[128,4096]{1,0:T(8,128)(2,1)S(1)} %copy-done.12, bf16[16,8,32,128]{3,2,1,0:T(8,128)(2,1)} %bitcast.309), kind=kOutput, calls=%fused_computation.178 | convolution fusion | flops 4296540160 | bytes 36700160 | tf_op jit(solution)/shard_map/dot_general | solution.py:401
  158.4 27.7 %fusion.121.clone.5 = bf16[256,7168]{1,0:T(8,128)(2,1)} fusion(bf16[2,4096,14336]{2,1,0:T(8,128)(2,1)} %param.60, s32[]{:T(128)S(6)} %select_n.365, bf16[128,4096]{1,0:T(8,128)(2,1)S(1)} %collective-permute-done.15, bf16[128,4096]{1,0:T(8,128)(2,1)S(1)} %fusion.141), kind=kOutput, calls=%fused_computation.170.clone.clone.clone.2 | convolution fusion | flops 15056764928 | bytes 64487428 | tf_op jit(solution)/shard_map/dot_general | solution.py:401
  186.1 25.2 %fusion.76 = f32[256,4096]{1,0:T(8,128)S(1)} fusion(bf16[2,14336,4096]{2,1,0:T(8,128)(2,1)} %param.61, s32[]{:T(128)S(6)} %select_n.365, bf16[256,7168]{1,0:T(8,128)(2,1)} %fusion.121.clone.5), kind=kOutput, calls=%fused_computation.123 | convolution fusion | flops 15032385536 | bytes 66584580 | tf_op jit(solution)/shard_map/dot_general | solution.py:401
  215.2 13.0 %all-reduce.6.cloned.1.call-done.moved.rest_1_ = bf16[2,1024,8,128]{3,2,1,0:T(8,128)(2,1)} async-done(((bf16[2,1024,8,128]{3,2,1,0:T(8,128)(2,1)}), bf16[2,1024,8,128]{3,2,1,0:T(8,128)(2,1)}) %all-reduce.6.cloned.1.call-update) | async-done | bytes 4194320 | tf_op jit(solution)/shard_map/psum | solution.py:553
  230.8 5.0 %fusion.193 = bf16[16,8,8,128]{3,1,2,0:T(8,128)(2,1)S(1)} fusion(bf16[128,4096]{1,0:T(8,128)(2,1)S(1)} %fusion.162, bf16[2,4096,1024]{2,1,0:T(8,128)(2,1)} %param.58), kind=kOutput, calls=%fused_computation.215 | convolution fusion | flops 1073872896 | bytes 9699328 | tf_op jit(solution)/shard_map/dot_general | solution.py:401
  240.6 13.2 %fusion.175 = bf16[16,8,32,128]{3,1,2,0:T(8,128)(2,1)S(1)} fusion(bf16[128,4096]{1,0:T(8,128)(2,1)} %copy-done.14, bf16[2,4096,4096]{2,1,0:T(8,128)(2,1)} %param.56), kind=kOutput, calls=%fused_computation.205 | convolution fusion | flops 4295491584 | bytes 35651584 | tf_op jit(solution)/shard_map/dot_general | solution.py:401
  255.1 23.1 %shard_map.170 = bf16[64,2,32,128]{3,2,1,0:T(8,128)(2,1)} custom-call(s32[5,64]{1,0:T(8,128)} %get-tuple-element.872.meta, bf16[64,2,32,128]{3,2,1,0:T(8,128)(2,1)} %bitcast.308, bf16[64,2,2,8,128]{4,3,2,1,0:T(8,128)(2,1)S(1)} %maximum_bitcast_fusion.1.new_ref.rest_3_, bf16[192,2,16,8,128]{4,3,2,1,0:T(8,128)(2,1)} %get-tuple-element.1098, ...), custom_call_target="tpu_custom_call" | custom-call | flops 10000000000 | bytes 10000000 | tf_op jit(solution)/shard_map/pallas_call | solution.py:261
  278.3 13.8 %add_convert_fusion = bf16[128,4096]{1,0:T(8,128)(2,1)S(1)} fusion(bf16[128,4096]{1,0:T(8,128)(2,1)} %copy-done.14, bf16[2,4096,4096]{2,1,0:T(8,128)(2,1)} %param.59, bf16[16,8,32,128]{3,2,1,0:T(8,128)(2,1)} %bitcast.310), kind=kOutput, calls=%fused_computation.204 | convolution fusion | flops 4296540160 | bytes 36700160 | tf_op jit(solution)/shard_map/dot_general | solution.py:401
  294.9 25.2 %fusion.133.clone.5 = bf16[256,7168]{1,0:T(8,128)(2,1)} fusion(bf16[2,4096,14336]{2,1,0:T(8,128)(2,1)} %param.60, s32[]{:T(128)S(6)} %select_n.365, bf16[128,4096]{1,0:T(8,128)(2,1)} %collective-permute-done.18, bf16[128,4096]{1,0:T(8,128)(2,1)S(1)} %add_convert_fusion), kind=kOutput, calls=%fused_computation.176.clone.clone.clone.2 | convolution fusion | flops 15056764928 | bytes 64487428 | tf_op jit(solution)/shard_map/dot_general | solution.py:401
  320.3 27.0 %fusion.72 = f32[256,4096]{1,0:T(8,128)} fusion(bf16[2,14336,4096]{2,1,0:T(8,128)(2,1)} %param.61, s32[]{:T(128)S(6)} %select_n.365, bf16[256,7168]{1,0:T(8,128)(2,1)} %fusion.133.clone.5), kind=kOutput, calls=%fused_computation.119 | convolution fusion | flops 15032385536 | bytes 66584580 | tf_op jit(solution)/shard_map/dot_general | solution.py:401
  351.2 23.3 %collective-permute-start.21 = (bf16[64,2,2,8,128]{4,3,2,1,0:T(8,128)(2,1)S(1)}, bf16[64,2,2,8,128]{4,3,2,1,0:T(8,128)(2,1)S(1)}, u32[]{:S(2)}, u32[]{:S(2)}) collective-permute-start(bf16[64,2,2,8,128]{4,3,2,1,0:T(8,128)(2,1)S(1)} %copy-done.6), channel_id=1, source_target_pairs={{0,1},{1,2},{2,3},{3,4},{4,5},{5,6},{6,7},{7,0}} | collective-permute-start | bytes 1572872 | tf_op jit(solution)/shard_map/ppermute | solution.py:543
  376.0 18.5 %collective-permute-done.20.rest_4_ = bf16[64,2,2,8,128]{4,3,2,1,0:T(8,128)(2,1)S(1)} collective-permute-done((bf16[64,2,2,8,128]{4,3,2,1,0:T(8,128)(2,1)S(1)}, bf16[64,2,2,8,128]{4,3,2,1,0:T(8,128)(2,1)S(1)}, u32[]{:S(2)}, u32[]{:S(2)}) %collective-permute-start.20) | collective-permute-done | bytes 524320 | tf_op jit(solution)/shard_map/ppermute | solution.py:543
  403.0 17.6 %finish_pools.1 = (bf16[192,2,16,8,128]{4,3,2,1,0:T(8,128)(2,1)}, bf16[192,2,16,8,128]{4,3,2,1,0:T(8,128)(2,1)}) custom-call(s32[2,64]{1,0:T(2,128)} %pad_add_fusion.4.mig, s32[3,192]{1,0:T(4,128)} %broadcast_add_fusion.owner, bf16[192,2,16,8,128]{4,3,2,1,0:T(8,128)(2,1)} %get-tuple-element.438.k_in, ...), custom_call_target="tpu_custom_call", output_to_operand_aliasing={{0}: (2, {}), {1}: (3, {})} | custom-call | tf_op jit(solution)/shard_map/finish_pools/pallas_call | solution.py:378
  424.1 13.6 %conditional.27 = (bf16[2,64,4096]{2,1,0:T(8,128)(2,1)S(1)}) conditional(s32[]{:T(128)} %convert_element_type.209, bf16[2,64,4096]{2,1,0:T(8,128)(2,1)S(1)} %get-tuple-element.1082, (s32[64]{0:T(128)S(1)}, pred[64,64]{0,1:T(32,128)(4,1)S(1)}, bf16[64,2,4096]{2,1,0:T(2,128)(2,1)S(1)}, bf16[2,64,4096]{2,1,0:T(8,128)(2,1)S(1)}) %tuple.388), branch_computations={%region_52.54_spmd, %region_53.55_spmd} | conditional | flops 68161600 | bytes 9441712 | solution.py:574
  424.7 12.3 %collective-permute-done.7 = bf16[64,2,4096]{2,0,1:T(8,128)(2,1)S(1)} collective-permute-done((bf16[64,2,4096]{2,0,1:T(8,128)(2,1)S(1)}, bf16[64,2,4096]{2,0,1:T(8,128)(2,1)S(1)}, u32[]{:S(2)}, u32[]{:S(2)}) %collective-permute-start.7) | collective-permute-done | bytes 1048608 | tf_op jit(solution)/shard_map/cond/branch_1_fun/ppermute | solution.py:568
  (213 shorter events, 60.5 us)
Async XLA Ops:
  7.2 109.9 %all-reduce.4.cloned.1.call-start = ((), (), s32[]{:S(2)}) async-start(), calls=%async_computation.2 | async-start | bytes 5505024 | tf_op jit(solution)/shard_map/psum | solution.py:476
  17.4 65.2 %copy-start.19 = (s32[512,2]{0,1:T(2,128)}, s32[512,2]{0,1:T(2,128)S(1)}, u32[]{:S(2)}) copy-start(s32[512,2]{0,1:T(2,128)S(1)} %and_select_fusion.5) | copy-start | bytes 12292
  18.2 32.6 %copy-start.23 = (s32[512]{0:T(512)}, s32[512]{0:T(512)S(1)}, u32[]{:S(2)}) copy-start(s32[512]{0:T(512)S(1)} %convert_reduce_fusion.3) | copy-start | bytes 6148
  19.0 34.2 %copy-start.38 = (s32[64]{0:T(128)}, s32[64]{0:T(128)S(1)}, u32[]{:S(2)}) copy-start(s32[64]{0:T(128)S(1)} %and_select_fusion.10) | copy-start | bytes 772
  19.3 32.8 %copy-start.21 = (s32[512]{0:T(512)}, s32[512]{0:T(512)S(1)}, u32[]{:S(2)}) copy-start(s32[512]{0:T(512)S(1)} %convert_reduce_fusion) | copy-start | bytes 6148
  25.5 24.8 %collective-permute-start = (bf16[64,2,4096]{2,0,1:T(8,128)(2,1)S(1)}, bf16[64,2,4096]{2,0,1:T(8,128)(2,1)S(1)}, u32[]{:S(2)}, u32[]{:S(2)}) collective-permute-start(bf16[64,2,4096]{2,0,1:T(8,128)(2,1)S(1)} %convolution_convert_fusion.1), channel_id=1, source_target_pairs={{0,1},{1,2},{2,3},{3,4},{4,5},{5,6},{6,7},{7,0}} | collective-permute-start | bytes 3145736 | tf_op jit(solution)/shard_map/cond/branch_1_fun/ppermute | solution.py:507
  64.4 52.7 %collective-permute-start.14 = (bf16[2,608,8,128]{3,2,1,0:T(8,128)(2,1)}, bf16[2,608,8,128]{3,2,1,0:T(8,128)(2,1)}, u32[]{:S(2)}, u32[]{:S(2)}) collective-permute-start(bf16[2,608,8,128]{3,2,1,0:T(8,128)(2,1)} %get-tuple-element.430), channel_id=1, source_target_pairs={{0,7},{1,0},{2,1},{3,2},{4,3},{5,4},{6,5},{7,6}} | collective-permute-start | bytes 7471112 | tf_op jit(solution)/shard_map/ppermute | solution.py:515
  116.2 176.6 %copy-start.2 = (bf16[64,2,2,8,128]{4,3,2,1,0:T(8,128)(2,1)}, bf16[64,2,2,8,128]{4,3,2,1,0:T(8,128)(2,1)S(1)}, u32[]{:S(2)}) copy-start(bf16[64,2,2,8,128]{4,3,2,1,0:T(8,128)(2,1)S(1)} %maximum_bitcast_fusion.new_ref.rest_2_) | copy-start | bytes 1572868
  117.7 110.5 %all-reduce.6.cloned.1.call-start = ((), (), s32[]{:S(2)}) async-start(), calls=%async_computation.3 | async-start | bytes 8388608 | tf_op jit(solution)/shard_map/psum | solution.py:553
  154.6 3.8 collective-permute-start.15
  214.7 13.5 %collective-permute-start.16 = (f32[128,4096]{1,0:T(8,128)}, f32[128,4096]{1,0:T(8,128)}, u32[]{:S(2)}, u32[]{:S(2)}) collective-permute-start(f32[128,4096]{1,0:T(8,128)} %slice.126), channel_id=1, source_target_pairs={{0,1},{1,0},{2,3},{3,2},{4,5},{5,4},{6,7},{7,6}} | collective-permute-start | bytes 6291464 | tf_op jit(solution)/shard_map/ppermute | solution.py:412
  214.8 40.3 %collective-permute-start.17 = (bf16[2,608,8,128]{3,2,1,0:T(8,128)(2,1)}, bf16[2,608,8,128]{3,2,1,0:T(8,128)(2,1)}, u32[]{:S(2)}, u32[]{:S(2)}) collective-permute-start(bf16[2,608,8,128]{3,2,1,0:T(8,128)(2,1)} %get-tuple-element.437), channel_id=1, source_target_pairs={{0,7},{1,0},{2,1},{3,2},{4,3},{5,4},{6,5},{7,6}} | collective-permute-start | bytes 7471112 | tf_op jit(solution)/shard_map/ppermute | solution.py:557
  255.1 37.7 %copy-start.5 = (bf16[64,2,2,8,128]{4,3,2,1,0:T(8,128)(2,1)}, bf16[64,2,2,8,128]{4,3,2,1,0:T(8,128)(2,1)S(1)}, u32[]{:S(2)}) copy-start(bf16[64,2,2,8,128]{4,3,2,1,0:T(8,128)(2,1)S(1)} %maximum_bitcast_fusion.1.new_ref.rest_3_) | copy-start | bytes 1572868
  292.1 2.8 collective-permute-start.18
  292.9 105.0 %all-reduce.8.cloned.1.call-start = ((), (), s32[]{:S(2)}) async-start(), calls=%async_computation.4 | async-start | bytes 8388608 | tf_op jit(solution)/shard_map/psum | solution.py:553
  320.2 30.9 %copy-start.28 = (s32[512,1]{0,1:T(1,128)S(1)}, s32[512,1]{0,1:T(1,128)}, u32[]{:S(2)}) copy-start(s32[512,1]{0,1:T(1,128)} %copy-done.27) | copy-start | bytes 6148
  320.2 31.0 %copy-start.6 = (bf16[64,2,2,8,128]{4,3,2,1,0:T(8,128)(2,1)S(1)}, bf16[64,2,2,8,128]{4,3,2,1,0:T(8,128)(2,1)}, u32[]{:S(2)}) copy-start(bf16[64,2,2,8,128]{4,3,2,1,0:T(8,128)(2,1)} %copy-done.5) | copy-start | bytes 1572868
  320.2 54.3 %copy-start.30 = (s32[64]{0:T(128)S(1)}, s32[64]{0:T(128)}, u32[]{:S(2)}) copy-start(s32[64]{0:T(128)} %get-tuple-element.866) | copy-start | bytes 772
  320.2 54.9 %copy-start.26 = (s32[512]{0:T(512)S(1)}, s32[512]{0:T(512)}, u32[]{:S(2)}) copy-start(s32[512]{0:T(512)} %copy-done.25) | copy-start | bytes 6148
  320.2 55.1 %copy-start.36 = (s32[3]{0:T(128)S(1)}, s32[3]{0:T(128)}, u32[]{:S(2)}) copy-start(s32[3]{0:T(128)} %constant.247) | copy-start | bytes 40
  350.4 70.1 %collective-permute-start.19 = (f32[128,4096]{1,0:T(8,128)}, f32[128,4096]{1,0:T(8,128)}, u32[]{:S(2)}, u32[]{:S(2)}) collective-permute-start(f32[128,4096]{1,0:T(8,128)} %slice.129), channel_id=1, source_target_pairs={{0,1},{1,0},{2,3},{3,2},{4,5},{5,4},{6,7},{7,6}} | collective-permute-start | bytes 6291464 | tf_op jit(solution)/shard_map/ppermute | solution.py:412
  350.6 43.9 %collective-permute-start.20 = (bf16[64,2,2,8,128]{4,3,2,1,0:T(8,128)(2,1)S(1)}, bf16[64,2,2,8,128]{4,3,2,1,0:T(8,128)(2,1)S(1)}, u32[]{:S(2)}, u32[]{:S(2)}) collective-permute-start(bf16[64,2,2,8,128]{4,3,2,1,0:T(8,128)(2,1)S(1)} %copy-done.3), channel_id=1, source_target_pairs={{0,1},{1,2},{2,3},{3,4},{4,5},{5,6},{6,7},{7,0}} | collective-permute-start | bytes 1572872 | tf_op jit(solution)/shard_map/ppermute | solution.py:543
  351.2 50.9 %collective-permute-start.21 = (bf16[64,2,2,8,128]{4,3,2,1,0:T(8,128)(2,1)S(1)}, bf16[64,2,2,8,128]{4,3,2,1,0:T(8,128)(2,1)S(1)}, u32[]{:S(2)}, u32[]{:S(2)}) collective-permute-start(bf16[64,2,2,8,128]{4,3,2,1,0:T(8,128)(2,1)S(1)} %copy-done.6), channel_id=1, source_target_pairs={{0,1},{1,2},{2,3},{3,4},{4,5},{5,6},{6,7},{7,0}} | collective-permute-start | bytes 1572872 | tf_op jit(solution)/shard_map/ppermute | solution.py:543
  424.7 12.3 %collective-permute-start.7 = (bf16[64,2,4096]{2,0,1:T(8,128)(2,1)S(1)}, bf16[64,2,4096]{2,0,1:T(8,128)(2,1)S(1)}, u32[]{:S(2)}, u32[]{:S(2)}) collective-permute-start(bf16[64,2,4096]{2,0,1:T(8,128)(2,1)S(1)} %copy.123), channel_id=1, source_target_pairs={{0,7},{1,0},{2,1},{3,2},{4,3},{5,4},{6,5},{7,6}} | collective-permute-start | bytes 3145736 | tf_op jit(solution)/shard_map/cond/branch_1_fun/ppermute | solution.py:568
  (27 other events, 398.3 us)
Sparse Core Ops, SparseCore 0:
  17.1 66.1 all-reduce.3
  156.0 72.1 all-reduce.5
  296.9 100.8 all-reduce.7
where the time goes:
time: 455 us; the launch traced here: 446 us
  matrix products  179 us (39%)
  Pallas kernels  104 us (23%)
  waiting for transfers between devices  80.7 us (18%)
  starting transfers between devices  26.2 us (6%)
  between operations  21.1 us (5%)
  other arithmetic  17.3 us (4%)
  local copies, waits for them, and re-layouts  16.4 us (4%)
    dot_general x12, matrix products, dense(): return jnp.dot(hidden, weight, preferred_element_type=jnp.float32)  178 us
    pallas_call x2, Pallas kernels, attend(): pl.pallas_call(functools.partial(attend_kernel, layer, seqs, page_len, nu...  46 us
    ppermute x1, waiting for transfers between devices, send_embeds(): rows = lax.ppermute(rows, 'kv', shift_by(group_size, step_away))  24.8 us
    ppermute x2, starting transfers between devices, device_fn(): prev_rows.append(lax.ppermute(rows, 'kv', shift_by(group_size, 1)))  23.6 us
    ppermute x2, waiting for transfers between devices, device_fn(): prev_rows.append(lax.ppermute(rows, 'kv', shift_by(group_size, 1)))  22.8 us
    pallas_call x1, Pallas kernels, finish_pools(): pl.pallas_call(functools.partial(finish_kernel, layers, slots, entries),...  17.6 us
    pallas_call x1, Pallas kernels, copy_pools(): pl.pallas_call(copy_kernel, out_shape=[pool, pool], in_specs=[any_spec(),...  17.5 us
    psum x2, waiting for transfers between devices, device_fn(): moved.append(lax.psum(full_out[after], 'kv'))  16.3 us
  transfers between devices with their start and end apart: 13, of which 8 were waited for; matrix products, arithmetic and copies ran while one was open for 39% of the time, Pallas kernels for 12%

commit v1 on v0

--- a/solution.py
+++ b/solution.py
@@ -393,6 +393,7 @@
             pltpu.SemaphoreType.DMA((1,)),
             pltpu.SemaphoreType.DMA((1,)),
         ],
+        cost_estimate=pl.CostEstimate(flops=10 ** 10, bytes_accessed=10 ** 7, transcendentals=0),
         name='finish_pools',
     )(mig, owner, k_pool, v_pool, *moved, *own, *prev, *far)
 
@@ -458,8 +459,6 @@
         old_table = jnp.where(is_moved, masked_pick(remap, mig_src), new_table)
         page_src = old_table // slots
         page_slot = old_table % slots
-        dev, pos = place_sequences(page_src[:, 0], group_size, per_dev)
-        place = dev * per_dev + pos
 
         page_ids = jnp.arange(page_count, dtype=I32)[None, :]
         page_rows = jnp.where(page_ids == 0, page_len, seq_lens[:, None] - page_len)
@@ -473,7 +472,12 @@
         moved_first = excl_cumsum(moved_rows)
         moved_fits = moved_first + moved_rows <= moved_cap
         moved_meta = jnp.stack([jnp.where(moved_fits, clear_slot, -1), moved_first, moved_rows])
-        moved = [lax.psum(pack_rows((0,), k_pool, v_pool, moved_meta, moved_cap)[0], 'kv')]
+        moved_out = pack_rows((0,), k_pool, v_pool, moved_meta, moved_cap)[0]
+        moved_out, new_table, page_src, page_slot = lax.optimization_barrier((moved_out, new_table, page_src, page_slot))
+        moved = [lax.psum(moved_out, 'kv')]
+
+        dev, pos = place_sequences(page_src[:, 0], group_size, per_dev)
+        place = dev * per_dev + pos
 
         is_local = page_src == dev[:, None]
         in_moved = jnp.any(remap & moved_fits, axis=-1) & ~is_local
@@ -492,6 +496,7 @@
         other_shape = (per_dev * page_count, 2) + k_pool.shape[1:]
         far_shape = (seq_count, 2, STEPS, kv_heads, head_dim)
         *near_out, other, far_0, far_1 = pack_rows(tuple(range(layers)), k_pool, v_pool, near_meta, near_cap, [other_shape, far_shape, far_shape])
+        near_out[0], embeds = lax.optimization_barrier((near_out[0], embeds))
 
         my_dev = lax.dynamic_slice_in_dim(dev, me * per_dev, per_dev)
         my_pos = lax.dynamic_slice_in_dim(pos, me * per_dev, per_dev)
@@ -559,9 +564,8 @@
             hidden = (hidden.astype(jnp.float32) + dense(attn, w_out[layer])).astype(jnp.bfloat16)
             hidden = pair_mlp(hidden, w_up, w_down, layer, me % 2, pairs)
 
-        far_rows = [lax.cond(jnp.any(is_far), lambda own, far: lax.all_gather(own, 'kv', axis=0, tiled=True), lambda own, far: far, own, far) for own, far in zip(own_rows, (far_0, far_1))]
-        k_out, v_out = finish_pools(k_base, v_base, moved[1:], own_rows, prev_rows, far_rows, mig_meta, owner_meta)
-
+        hidden, moved[1], *far_in = lax.optimization_barrier((hidden, moved[1], *own_rows))
+        far_rows = lax.cond(jnp.any(is_far), lambda own, far: [lax.all_gather(rows, 'kv', axis=0, tiled=True) for rows in own], lambda own, far: far, far_in, [far_0, far_1])
         hidden = hidden.reshape(per_dev, STEPS, width)
 
         def bring_home(step_away, total):
@@ -569,9 +573,17 @@
             sel = (at_pos & (my_distance == step_away)[None, :]).astype(hidden.dtype)
             return total + jnp.einsum('pb,ptd->tbd', sel, rows, preferred_element_type=jnp.float32).astype(hidden.dtype)
 
-        y_out = jnp.zeros((STEPS, per_dev, width), hidden.dtype)
+        def bring_most(step_away, k_base, v_base):
+            rows = lax.ppermute(hidden, 'kv', shift_by(group_size, -step_away)) if step_away else hidden
+            k_out, v_out = finish_pools(k_base, v_base, moved[1:], own_rows, prev_rows, far_rows, mig_meta, owner_meta)
+            sel = (at_pos & (my_distance == step_away)[None, :]).astype(hidden.dtype)
+            return jnp.einsum('pb,ptd->tbd', sel, rows, preferred_element_type=jnp.float32).astype(hidden.dtype), k_out, v_out
+
+        counts = jnp.sum(distance[None, :] == jnp.arange(group_size, dtype=I32)[:, None], axis=1)
+        most = jnp.argmax(counts).astype(I32)
+        y_out, k_out, v_out = lax.switch(most, [functools.partial(bring_most, step_away) for step_away in range(group_size)], k_base, v_base)
         for step_away in range(group_size):
-            y_out = lax.cond(jnp.any(distance == step_away), functools.partial(bring_home, step_away), lambda same: same, y_out)
+            y_out = lax.cond((counts[step_away] > 0) & (most != step_away), functools.partial(bring_home, step_away), lambda same: same, y_out)
         return y_out, k_out, v_out
 
     return jax.shard_map(device_fn, mesh=mesh, in_specs=(tok_spec, P(), P(), P(), P(), P(), P(), pool_spec, pool_spec, P('rep', None), P('rep'), P('rep'), P('rep')), out_specs=(tok_spec, pool_spec, pool_spec), check_vma=False)

time: 455 us -> 525 us (1.15)
  waiting for transfers between devices: 80.7 us -> 113 us
  local copies, waits for them, and re-layouts: 16.4 us -> 31.4 us
  other arithmetic: 17.3 us -> 28.2 us
  between operations: 21.1 us -> 31 us
    psum x2, waiting for transfers between devices: 16.3 us -> 83.1 us  [device_fn(): moved.append(lax.psum(full_out[after], 'kv'))]
    ppermute x2, waiting for transfers between devices: 22.8 us -> 0.01 us  [device_fn(): prev_rows.append(lax.ppermute(rows, 'kv', shift_by(group_size, 1)))]
    ppermute x1, waiting for transfers between devices: 12.3 us -> 0.01 us  [bring_most(): lax.ppermute(hidden, 'kv', shift_by(group_size, -step_away))]
    psum x1, waiting for transfers between devices: 0.01 us -> 9.67 us  [device_fn(): moved = [lax.psum(moved_out, 'kv')]]
    ppermute x1, waiting for transfers between devices: 24.8 us -> 15.1 us  [send_embeds(): rows = lax.ppermute(rows, 'kv', shift_by(group_size, step_away))]
    unnamed x83 -> x113, local copies, waits for them, and re-layouts: 6.77 us -> 13.5 us
  transfers between devices with their start and end apart: 13 -> 13, of which waited for: 8 -> 6; matrix products, arithmetic and copies ran while one was open for 39% -> 26% of each run, Pallas kernels for 12% -> 8%
where the time goes in v1:
time: 525 us; the launch traced here: 515 us
  matrix products  180 us (34%)
  waiting for transfers between devices  113 us (22%)
  Pallas kernels  104 us (20%)
  local copies, waits for them, and re-layouts  31.4 us (6%)
  between operations  31 us (6%)
  other arithmetic  28.2 us (5%)
  starting transfers between devices  25.9 us (5%)
    dot_general x12, matrix products, dense(): return jnp.dot(hidden, weight, preferred_element_type=jnp.float32)  178 us
    psum x2, waiting for transfers between devices, device_fn(): moved.append(lax.psum(full_out[after], 'kv'))  83.1 us
    pallas_call x2, Pallas kernels, attend(): pl.pallas_call(functools.partial(attend_kernel, layer, seqs, page_len, nu...  46.2 us
    ppermute x2, starting transfers between devices, device_fn(): prev_rows.append(lax.ppermute(rows, 'kv', shift_by(group_size, 1)))  22.9 us
    pallas_call x1, Pallas kernels, copy_pools(): pl.pallas_call(copy_kernel, out_shape=[pool, pool], in_specs=[any_spec(),...  17.8 us
    pallas_call x1, Pallas kernels, finish_pools(): pl.pallas_call(functools.partial(finish_kernel, layers, slots, entries),...  17.4 us
    pallas_call x2, Pallas kernels, pack_rows(): pl.pallas_call(functools.partial(pack_rows_kernel, layers), out_shape=out...  15.6 us
    ppermute x1, waiting for transfers between devices, send_embeds(): rows = lax.ppermute(rows, 'kv', shift_by(group_size, step_away))  15.1 us
  transfers between devices with their start and end apart: 13, of which 6 were waited for; matrix products, arithmetic and copies ran while one was open for 26% of the time, Pallas kernels for 8%

profile of v1, /device:TPU:0, one launch (start us, length us, event | category | flops | bytes accessed | tf_op | source)
XLA Modules:
  0.0 515.0 jit_solution(16865544102104622251)
XLA Ops:
  14.4 6.1 %shard_map.166 = bf16[2,672,8,128]{3,2,1,0:T(8,128)(2,1)} custom-call(s32[3,64]{1,0:T(4,128)} %pad_add_fusion.3.meta, bf16[192,2,16,8,128]{4,3,2,1,0:T(8,128)(2,1)} %k_pool.10, bf16[192,2,16,8,128]{4,3,2,1,0:T(8,128)(2,1)} %v_pool.10), custom_call_target="tpu_custom_call" | custom-call | tf_op jit(solution)/shard_map/pallas_call | solution.py:164
  26.0 9.5 %shard_map.167 = (bf16[2,608,8,128]{3,2,1,0:T(8,128)(2,1)}, bf16[2,608,8,128]{3,2,1,0:T(8,128)(2,1)}, bf16[128,2,2,16,8,128]{5,4,3,2,1,0:T(8,128)(2,1)}, bf16[51...) custom-call(s32[3,64]{1,0:T(4,128)} %broadcast_add_fusion.2.meta, bf16[192,2,16,8,128]{4,3,2,1,0:T(8,128)(2,1)} %k_pool.10, ...), custom_call_target="tpu_custom_call" | custom-call | tf_op jit(solution)/shard_map/pallas_call | solution.py:164
  37.0 16.2 %conditional.35 = (bf16[64,2,4096]{2,0,1:T(8,128)(2,1)S(1)}) conditional(s32[]{:T(128)} %convert_element_type.311, bf16[64,2,4096]{2,0,1:T(8,128)(2,1)S(1)} %get-tuple-element.2147, (s32[64]{0:T(128)S(1)}, pred[64,64]{0,1:T(32,128)(4,1)S(1)}, bf16[2,64,4096]{2,1,0:T(8,128)(2,1)S(1)}, bf16[64,2,4096]{2,0,1:T(8,128)(2,1)S(1)}) %tuple.505), branch_computations={%region_25.26_spmd, %region_26.27_spmd} | conditional | flops 68161600 | bytes 9449904 | solution.py:517
  37.6 15.1 %collective-permute-done = bf16[64,2,4096]{2,0,1:T(8,128)(2,1)S(1)} collective-permute-done((bf16[64,2,4096]{2,0,1:T(8,128)(2,1)S(1)}, bf16[64,2,4096]{2,0,1:T(8,128)(2,1)S(1)}, u32[]{:S(2)}, u32[]{:S(2)}) %collective-permute-start) | collective-permute-done | bytes 1048608 | tf_op jit(solution)/shard_map/cond/branch_1_fun/ppermute | solution.py:512
  66.9 5.5 %fusion.236 = bf16[16,8,8,128]{3,1,2,0:T(8,128)(2,1)} fusion(bf16[128,4096]{1,0:T(8,128)(2,1)S(1)} %reshape.701, bf16[2,4096,1024]{2,1,0:T(8,128)(2,1)} %param.63), kind=kOutput, calls=%fused_computation.268 | convolution fusion | flops 1073872896 | bytes 9699328 | tf_op jit(solution)/shard_map/dot_general | solution.py:402
  72.3 14.3 %fusion.212 = bf16[16,8,32,128]{3,1,2,0:T(8,128)(2,1)} fusion(bf16[128,4096]{1,0:T(8,128)(2,1)S(1)} %reshape.701, bf16[2,4096,4096]{2,1,0:T(8,128)(2,1)} %param.62), kind=kOutput, calls=%fused_computation.256 | convolution fusion | flops 4295491584 | bytes 35651584 | tf_op jit(solution)/shard_map/dot_general | solution.py:402
  100.7 17.8 %copy_pools.1 = (bf16[192,2,16,8,128]{4,3,2,1,0:T(8,128)(2,1)}, bf16[192,2,16,8,128]{4,3,2,1,0:T(8,128)(2,1)}) custom-call(bf16[192,2,16,8,128]{4,3,2,1,0:T(8,128)(2,1)} %k_pool.10, bf16[192,2,16,8,128]{4,3,2,1,0:T(8,128)(2,1)} %v_pool.10), custom_call_target="tpu_custom_call" | custom-call | tf_op jit(solution)/shard_map/copy_pools/pallas_call | solution.py:294
  118.6 7.3 %shard_map.168 = (bf16[2,1024,8,128]{3,2,1,0:T(8,128)(2,1)}, bf16[2,1024,8,128]{3,2,1,0:T(8,128)(2,1)}) custom-call(s32[1,64]{1,0:T(1,128)} %bitcast.394, bf16[192,2,16,8,128]{4,3,2,1,0:T(8,128)(2,1)} %k_pool.10, bf16[192,2,16,8,128]{4,3,2,1,0:T(8,128)(2,1)} %v_pool.10), custom_call_target="tpu_custom_call" | custom-call | tf_op jit(solution)/shard_map/pallas_call | solution.py:112
  128.7 9.7 %all-reduce.4.cloned.1.call-done.moved = bf16[2,672,8,128]{3,2,1,0:T(8,128)(2,1)} async-done(((bf16[2,672,8,128]{3,2,1,0:T(8,128)(2,1)}), bf16[2,672,8,128]{3,2,1,0:T(8,128)(2,1)}) %all-reduce.4.cloned.1.call-update) | async-done | bytes 2752528 | tf_op jit(solution)/shard_map/psum | solution.py:477
  140.5 23.1 %shard_map.169 = bf16[64,2,32,128]{3,2,1,0:T(8,128)(2,1)} custom-call(s32[5,64]{1,0:T(8,128)} %get-tuple-element.1903.meta, bf16[64,2,32,128]{3,2,1,0:T(8,128)(2,1)} %bitcast.363, bf16[64,2,2,8,128]{4,3,2,1,0:T(8,128)(2,1)} %maximum_bitcast_fusion.new_ref, bf16[192,2,16,8,128]{4,3,2,1,0:T(8,128)(2,1)} %get-tuple-element.2169, ...), custom_call_target="tpu_custom_call" | custom-call | flops 10000000000 | bytes 10000000 | tf_op jit(solution)/shard_map/pallas_call | solution.py:261
  163.7 13.5 %fusion.175 = bf16[128,4096]{1,0:T(8,128)(2,1)S(1)} fusion(bf16[2,4096,4096]{2,1,0:T(8,128)(2,1)} %param.65, bf16[128,4096]{1,0:T(8,128)(2,1)S(1)} %copy-done.8, bf16[16,8,32,128]{3,2,1,0:T(8,128)(2,1)} %bitcast.365), kind=kOutput, calls=%fused_computation.228 | convolution fusion | flops 4296540160 | bytes 36700160 | tf_op jit(solution)/shard_map/dot_general | solution.py:402
  179.8 27.7 %fusion.155.clone.5 = bf16[256,7168]{1,0:T(8,128)(2,1)} fusion(bf16[2,4096,14336]{2,1,0:T(8,128)(2,1)} %param.66, s32[]{:T(128)S(6)} %select_n.390, bf16[128,4096]{1,0:T(8,128)(2,1)S(1)} %collective-permute-done.22, bf16[128,4096]{1,0:T(8,128)(2,1)S(1)} %fusion.175), kind=kOutput, calls=%fused_computation.220.clone.clone.clone.2 | convolution fusion | flops 15056764928 | bytes 64487428 | tf_op jit(solution)/shard_map/dot_general | solution.py:402
  207.5 24.9 %fusion.110 = f32[256,4096]{1,0:T(8,128)S(1)} fusion(bf16[2,14336,4096]{2,1,0:T(8,128)(2,1)} %param.67, s32[]{:T(128)S(6)} %select_n.390, bf16[256,7168]{1,0:T(8,128)(2,1)} %fusion.155.clone.5), kind=kOutput, calls=%fused_computation.173 | convolution fusion | flops 15032385536 | bytes 66584580 | tf_op jit(solution)/shard_map/dot_general | solution.py:402
  237.0 13.2 %all-reduce.6.cloned.1.call-done.moved = bf16[2,1024,8,128]{3,2,1,0:T(8,128)(2,1)} async-done(((bf16[2,1024,8,128]{3,2,1,0:T(8,128)(2,1)}), bf16[2,1024,8,128]{3,2,1,0:T(8,128)(2,1)}) %all-reduce.6.cloned.1.call-update) | async-done | bytes 4194320 | tf_op jit(solution)/shard_map/psum | solution.py:558
  252.8 5.0 fusion.230
  264.0 13.4 %fusion.209 = bf16[16,8,32,128]{3,1,2,0:T(8,128)(2,1)S(1)} fusion(bf16[128,4096]{1,0:T(8,128)(2,1)} %copy-done.12, bf16[2,4096,4096]{2,1,0:T(8,128)(2,1)} %param.62), kind=kOutput, calls=%fused_computation.255 | convolution fusion | flops 4295491584 | bytes 35651584 | tf_op jit(solution)/shard_map/dot_general | solution.py:402
  282.0 23.1 %shard_map.170 = bf16[64,2,32,128]{3,2,1,0:T(8,128)(2,1)} custom-call(s32[5,64]{1,0:T(8,128)} %get-tuple-element.1902.meta, bf16[64,2,32,128]{3,2,1,0:T(8,128)(2,1)} %bitcast.364, bf16[64,2,2,8,128]{4,3,2,1,0:T(8,128)(2,1)} %maximum_bitcast_fusion.1.new_ref, bf16[192,2,16,8,128]{4,3,2,1,0:T(8,128)(2,1)} %get-tuple-element.2169, ...), custom_call_target="tpu_custom_call" | custom-call | flops 10000000000 | bytes 10000000 | tf_op jit(solution)/shard_map/pallas_call | solution.py:261
  305.1 13.5 %add_convert_fusion = bf16[128,4096]{1,0:T(8,128)(2,1)S(1)} fusion(bf16[128,4096]{1,0:T(8,128)(2,1)S(1)} %copy-done.13, bf16[2,4096,4096]{2,1,0:T(8,128)(2,1)} %param.65, bf16[16,8,32,128]{3,2,1,0:T(8,128)(2,1)} %bitcast.366), kind=kOutput, calls=%fused_computation.254 | convolution fusion | flops 4296540160 | bytes 36700160 | tf_op jit(solution)/shard_map/dot_general | solution.py:402
  321.3 26.8 %fusion.167.clone.5 = bf16[256,7168]{1,0:T(8,128)(2,1)} fusion(bf16[2,4096,14336]{2,1,0:T(8,128)(2,1)} %param.66, s32[]{:T(128)S(6)} %select_n.390, bf16[128,4096]{1,0:T(8,128)(2,1)S(1)} %collective-permute-done.25, bf16[128,4096]{1,0:T(8,128)(2,1)S(1)} %add_convert_fusion), kind=kOutput, calls=%fused_computation.226.clone.clone.clone.2 | convolution fusion | flops 15056764928 | bytes 64487428 | tf_op jit(solution)/shard_map/dot_general | solution.py:402
  348.2 24.3 %fusion.106 = f32[256,4096]{1,0:T(8,128)S(1)} fusion(bf16[2,14336,4096]{2,1,0:T(8,128)(2,1)} %param.67, s32[]{:T(128)S(6)} %select_n.390, bf16[256,7168]{1,0:T(8,128)(2,1)} %fusion.167.clone.5), kind=kOutput, calls=%fused_computation.169 | convolution fusion | flops 15032385536 | bytes 66584580 | tf_op jit(solution)/shard_map/dot_general | solution.py:402
  388.6 22.8 %collective-permute-start.28 = (bf16[64,2,2,8,128]{4,3,2,1,0:T(8,128)(2,1)}, bf16[64,2,2,8,128]{4,3,2,1,0:T(8,128)(2,1)S(1)}, u32[]{:S(2)}, u32[]{:S(2)}) collective-permute-start(bf16[64,2,2,8,128]{4,3,2,1,0:T(8,128)(2,1)} %maximum_bitcast_fusion.1.new_ref), channel_id=1, source_target_pairs={{0,1},{1,2},{2,3},{3,4},{4,5},{5,6},{6,7},{7,0}} | collective-permute-start | bytes 1572872 | tf_op jit(solution)/shard_map/ppermute | solution.py:548
  414.4 69.9 %all-reduce.8.cloned.1.call-done = bf16[2,1024,8,128]{3,2,1,0:T(8,128)(2,1)} async-done(((bf16[2,1024,8,128]{3,2,1,0:T(8,128)(2,1)}), bf16[2,1024,8,128]{3,2,1,0:T(8,128)(2,1)}) %all-reduce.8.cloned.1.call-update) | async-done | bytes 4194320 | tf_op jit(solution)/shard_map/psum | solution.py:558
  485.1 22.8 %conditional.43 = (bf16[192,2,16,8,128]{4,3,2,1,0:T(8,128)(2,1)}, bf16[192,2,16,8,128]{4,3,2,1,0:T(8,128)(2,1)}, bf16[2,64,4096]{2,1,0:T(8,128)(2,1)}, bf16[2,64,4096]{2,1,0:T(8,128)(2,1)S(1)}) conditional(s32[]{:T(128)} %clamp.3, (s32[2,64]{1,0:T(2,128)S(1)}, s32[3,192]{1,0:T(4,128)S(1)}, ...), branch_computations={%region_57.59_spmd, %region_58.60_spmd, %region_59.61_spmd, %regio... | conditional | flops 10067637248 | bytes 20490312
  487.5 17.4 %finish_pools.9 = (bf16[192,2,16,8,128]{4,3,2,1,0:T(8,128)(2,1)}, bf16[192,2,16,8,128]{4,3,2,1,0:T(8,128)(2,1)}) custom-call(s32[2,64]{1,0:T(2,128)S(1)} %get-tuple-element.631.mig, s32[3,192]{1,0:T(4,128)S(1)} %get-tuple-element.632.owner, bf16[192,2,16,8,128]{4,3,2,1,0:T(8,128)(2,1)} %get-tuple-element.633.k_in, ...), custom_call_target="tpu_custom_call", output_to_operand_aliasing={{0}: (2, {}), {1}: (3, {})} | custom-call | flops 10000000000 | bytes 10000000 | tf_op jit(solution)/shard_map/cond/branch_1_fun/finish_pools/pallas_call | solution.py:378
  (245 shorter events, 79.9 us)
Async XLA Ops:
  7.2 131.2 %all-reduce.4.cloned.1.call-start = ((), (), s32[]{:S(2)}) async-start(), calls=%async_computation.2 | async-start | bytes 5505024 | tf_op jit(solution)/shard_map/psum | solution.py:477
  13.8 48.8 %copy-start.15 = (s32[512,2]{0,1:T(2,128)}, s32[512,2]{0,1:T(2,128)S(1)}, u32[]{:S(2)}) copy-start(s32[512,2]{0,1:T(2,128)S(1)} %get-tuple-element.826) | copy-start | bytes 12292
  24.4 37.4 %copy-start.24 = (s32[512]{0:T(512)}, s32[512]{0:T(512)S(1)}, u32[]{:S(2)}) copy-start(s32[512]{0:T(512)S(1)} %select_reduce_fusion.3) | copy-start | bytes 6148
  37.5 15.1 %collective-permute-start = (bf16[64,2,4096]{2,0,1:T(8,128)(2,1)S(1)}, bf16[64,2,4096]{2,0,1:T(8,128)(2,1)S(1)}, u32[]{:S(2)}, u32[]{:S(2)}) collective-permute-start(bf16[64,2,4096]{2,0,1:T(8,128)(2,1)S(1)} %convolution_convert_fusion.1), channel_id=1, source_target_pairs={{0,1},{1,2},{2,3},{3,4},{4,5},{5,6},{6,7},{7,0}} | collective-permute-start | bytes 3145736 | tf_op jit(solution)/shard_map/cond/branch_1_fun/ppermute | solution.py:512
  58.7 36.1 %copy-start.7 = (bf16[128,4096]{1,0:T(8,128)(2,1)}, bf16[128,4096]{1,0:T(8,128)(2,1)S(1)}, u32[]{:S(2)}) copy-start(bf16[128,4096]{1,0:T(8,128)(2,1)S(1)} %reshape.701) | copy-start | bytes 3145732
  58.7 79.6 %collective-permute-start.21 = (bf16[2,608,8,128]{3,2,1,0:T(8,128)(2,1)}, bf16[2,608,8,128]{3,2,1,0:T(8,128)(2,1)S(1)}, u32[]{:S(2)}, u32[]{:S(2)}) collective-permute-start(bf16[2,608,8,128]{3,2,1,0:T(8,128)(2,1)} %get-tuple-element.846), channel_id=1, source_target_pairs={{0,7},{1,0},{2,1},{3,2},{4,3},{5,4},{6,5},{7,6}} | collective-permute-start | bytes 7471112 | tf_op jit(solution)/shard_map/ppermute | solution.py:520
  140.5 109.7 %all-reduce.6.cloned.1.call-start = ((), (), s32[]{:S(2)}) async-start(), calls=%async_computation.3 | async-start | bytes 8388608 | tf_op jit(solution)/shard_map/psum | solution.py:558
  177.1 2.7 collective-permute-start.22
  177.2 307.1 %all-reduce.8.cloned.1.call-start = ((), (), s32[]{:S(2)}) async-start(), calls=%async_computation.4 | async-start | bytes 8388608 | tf_op jit(solution)/shard_map/psum | solution.py:558
  235.9 14.3 %collective-permute-start.23 = (f32[128,4096]{1,0:T(8,128)}, f32[128,4096]{1,0:T(8,128)}, u32[]{:S(2)}, u32[]{:S(2)}) collective-permute-start(f32[128,4096]{1,0:T(8,128)} %slice.155), channel_id=1, source_target_pairs={{0,1},{1,0},{2,3},{3,2},{4,5},{5,4},{6,7},{7,6}} | collective-permute-start | bytes 6291464 | tf_op jit(solution)/shard_map/ppermute | solution.py:413
  235.9 44.6 %collective-permute-start.24 = (bf16[2,608,8,128]{3,2,1,0:T(8,128)(2,1)}, bf16[2,608,8,128]{3,2,1,0:T(8,128)(2,1)S(1)}, u32[]{:S(2)}, u32[]{:S(2)}) collective-permute-start(bf16[2,608,8,128]{3,2,1,0:T(8,128)(2,1)} %get-tuple-element.853), channel_id=1, source_target_pairs={{0,7},{1,0},{2,1},{3,2},{4,3},{5,4},{6,5},{7,6}} | collective-permute-start | bytes 7471112 | tf_op jit(solution)/shard_map/ppermute | solution.py:562
  318.6 2.7 collective-permute-start.25
  348.2 36.8 %copy-start.47 = (s32[64]{0:T(128)S(1)}, s32[64]{0:T(128)}, u32[]{:S(2)}) copy-start(s32[64]{0:T(128)} %param.73) | copy-start | bytes 772
  348.2 36.8 %copy-start.16 = (s32[512,2]{0,1:T(2,128)S(1)}, s32[512,2]{0,1:T(2,128)}, u32[]{:S(2)}) copy-start(s32[512,2]{0,1:T(2,128)} %copy-done.15) | copy-start | bytes 12292
  348.2 36.9 %copy-start.19 = (s32[512,2]{0,1:T(2,128)S(1)}, s32[512,2]{0,1:T(2,128)}, u32[]{:S(2)}) copy-start(s32[512,2]{0,1:T(2,128)} %param.70) | copy-start | bytes 12292
  348.2 36.9 %copy-start.23 = (s32[512]{0:T(512)S(1)}, s32[512]{0:T(512)}, u32[]{:S(2)}) copy-start(s32[512]{0:T(512)} %copy-done.22) | copy-start | bytes 6148
  348.2 36.9 %copy-start.31 = (s32[512]{0:T(512)S(1)}, s32[512]{0:T(512)}, u32[]{:S(2)}) copy-start(s32[512]{0:T(512)} %copy-done.30) | copy-start | bytes 6148
  348.2 36.9 %copy-start.49 = (pred[512]{0:T(512)(128)(4,1)S(1)}, pred[512]{0:T(512)(128)(4,1)}, u32[]{:S(2)}) copy-start(pred[512]{0:T(512)(128)(4,1)} %copy-done.48) | copy-start | bytes 1540
  375.3 109.8 %copy-start.2 = (pred[64,64]{0,1:T(32,128)(4,1)S(1)}, pred[64,64]{0,1:T(32,128)(4,1)}, u32[]{:S(2)}) copy-start(pred[64,64]{0,1:T(32,128)(4,1)} %copy-done.1) | copy-start | bytes 12292
  375.3 109.8 %copy-start.55 = (s32[64]{0:T(128)S(1)}, s32[64]{0:T(128)}, u32[]{:S(2)}) copy-start(s32[64]{0:T(128)} %copy-done.54) | copy-start | bytes 772
  375.3 36.2 %collective-permute-start.26 = (f32[128,4096]{1,0:T(8,128)}, f32[128,4096]{1,0:T(8,128)}, u32[]{:S(2)}, u32[]{:S(2)}) collective-permute-start(f32[128,4096]{1,0:T(8,128)} %slice.158), channel_id=1, source_target_pairs={{0,1},{1,0},{2,3},{3,2},{4,5},{5,4},{6,7},{7,6}} | collective-permute-start | bytes 6291464 | tf_op jit(solution)/shard_map/ppermute | solution.py:413
  375.7 109.3 %collective-permute-start.27 = (bf16[64,2,2,8,128]{4,3,2,1,0:T(8,128)(2,1)}, bf16[64,2,2,8,128]{4,3,2,1,0:T(8,128)(2,1)S(1)}, u32[]{:S(2)}, u32[]{:S(2)}) collective-permute-start(bf16[64,2,2,8,128]{4,3,2,1,0:T(8,128)(2,1)} %maximum_bitcast_fusion.new_ref), channel_id=1, source_target_pairs={{0,1},{1,2},{2,3},{3,4},{4,5},{5,6},{6,7},{7,0}} | collective-permute-start | bytes 1572872 | tf_op jit(solution)/shard_map/ppermute | solution.py:548
  388.6 96.4 %collective-permute-start.28 = (bf16[64,2,2,8,128]{4,3,2,1,0:T(8,128)(2,1)}, bf16[64,2,2,8,128]{4,3,2,1,0:T(8,128)(2,1)S(1)}, u32[]{:S(2)}, u32[]{:S(2)}) collective-permute-start(bf16[64,2,2,8,128]{4,3,2,1,0:T(8,128)(2,1)} %maximum_bitcast_fusion.1.new_ref), channel_id=1, source_target_pairs={{0,1},{1,2},{2,3},{3,4},{4,5},{5,6},{6,7},{7,0}} | collective-permute-start | bytes 1572872 | tf_op jit(solution)/shard_map/ppermute | solution.py:548
  486.6 18.3 %collective-permute-start.7 = (bf16[64,2,4096]{2,0,1:T(8,128)(2,1)}, bf16[64,2,4096]{2,0,1:T(8,128)(2,1)S(1)}, u32[]{:S(2)}, u32[]{:S(2)}) collective-permute-start(bf16[64,2,4096]{2,0,1:T(8,128)(2,1)} %copy.169), channel_id=1, source_target_pairs={{0,7},{1,0},{2,1},{3,2},{4,3},{5,4},{6,5},{7,6}} | collective-permute-start | bytes 3145736 | tf_op jit(solution)/shard_map/cond/branch_1_fun/ppermute | solution.py:577
  (42 other events, 449.0 us)
Sparse Core Ops, SparseCore 0:
  58.9 79.3 all-reduce.3
  177.3 72.8 all-reduce.5
  385.2 99.0 all-reduce.7

commit v2 on v1

--- a/solution.py
+++ b/solution.py
@@ -115,6 +115,7 @@
         in_specs=[smem_spec(), any_spec(), any_spec()],
         out_specs=[any_spec()] * len(layers),
         scratch_shapes=[pltpu.VMEM((len(layers),) + shape, k_pool.dtype), pltpu.SemaphoreType.DMA((len(layers),)), pltpu.SemaphoreType.DMA((len(layers),))],
+        cost_estimate=pl.CostEstimate(flops=10 ** 10, bytes_accessed=10 ** 7, transcendentals=0),
     )(slot_of[None, :].astype(I32), k_pool, v_pool)
 
 
@@ -172,7 +173,15 @@
             pltpu.SemaphoreType.DMA((len(layers),)),
             pltpu.SemaphoreType.DMA((len(layers),)),
         ],
+        cost_estimate=pl.CostEstimate(flops=10 ** 10, bytes_accessed=10 ** 7, transcendentals=0),
     )(meta.astype(I32), k_pool, v_pool)
+
+
+def gate(value):
+    def kernel(src, dst):
+        dst[...] = src[...]
+
+    return pl.pallas_call(kernel, out_shape=jax.ShapeDtypeStruct(value.shape, value.dtype), name='gate')(value)
 
 
 LOCAL, MOVED, NEXT, OTHER = range(4)
@@ -297,6 +306,7 @@
         in_specs=[any_spec(), any_spec()],
         out_specs=[any_spec(), any_spec()],
         scratch_shapes=[pltpu.VMEM((2,) + k_pool.shape, k_pool.dtype), pltpu.SemaphoreType.DMA((2, chunks)), pltpu.SemaphoreType.DMA((2, chunks))],
+        cost_estimate=pl.CostEstimate(flops=10 ** 10, bytes_accessed=10 ** 7, transcendentals=0),
         name='copy_pools',
     )(k_pool, v_pool)
 
@@ -409,9 +419,12 @@
     both = jnp.concatenate([hidden, lax.ppermute(hidden, 'kv', pairs)])
     up_proj = dense(both, lax.dynamic_slice(w_up, (layer, 0, core * half), (1, width, half))[0]).astype(jnp.bfloat16)
     act = jax.nn.gelu(up_proj.astype(jnp.float32), approximate=True).astype(jnp.bfloat16)
-    part = dense(act, lax.dynamic_slice(w_down, (layer, core * half, 0), (1, half, width))[0])
-    rest = lax.ppermute(part[rows:], 'kv', pairs)
-    return (hidden.astype(jnp.float32) + (part[:rows] + rest)).astype(jnp.bfloat16)
+    outs = []
+    for first in range(0, width, width // 2):
+        part = dense(act, lax.dynamic_slice(w_down, (layer, core * half, first), (1, half, width // 2))[0])
+        rest = lax.ppermute(part[rows:], 'kv', pairs)
+        outs.append((hidden[:, first:first + width // 2].astype(jnp.float32) + (part[:rows] + rest)).astype(jnp.bfloat16))
+    return jnp.concatenate(outs, axis=1)
 
 
 def shift_by(count, distance):
@@ -495,35 +508,48 @@
         near_meta = masked_pick(from_here[None, :, :], near_facts[:, None, :]) - jnp.array([[1], [0], [0]])
         other_shape = (per_dev * page_count, 2) + k_pool.shape[1:]
         far_shape = (seq_count, 2, STEPS, kv_heads, head_dim)
-        *near_out, other, far_0, far_1 = pack_rows(tuple(range(layers)), k_pool, v_pool, near_meta, near_cap, [other_shape, far_shape, far_shape])
-        near_out[0], embeds = lax.optimization_barrier((near_out[0], embeds))
-
         my_dev = lax.dynamic_slice_in_dim(dev, me * per_dev, per_dev)
         my_pos = lax.dynamic_slice_in_dim(pos, me * per_dev, per_dev)
         home = jnp.arange(seq_count, dtype=I32) // per_dev
         distance = (dev - home) % group_size
         my_distance = (my_dev - me) % group_size
         at_pos = my_pos[None, :] == jnp.arange(per_dev, dtype=I32)[:, None]
-
-        def send_embeds(step_away, hidden):
+        counts = jnp.sum(distance[None, :] == jnp.arange(group_size, dtype=I32)[:, None], axis=1)
+        most = jnp.argmax(counts).astype(I32)
+        all_same = counts[most] == seq_count
+
+        def send_embeds(step_away):
             sel = (at_pos & (my_distance == step_away)[None, :]).astype(embeds.dtype)
             rows = jnp.einsum('pb,tbd->ptd', sel, embeds, preferred_element_type=jnp.float32).astype(embeds.dtype)
-            if step_away:
-                rows = lax.ppermute(rows, 'kv', shift_by(group_size, step_away))
-            return hidden + rows
-
-        hidden = jnp.zeros((per_dev, STEPS, width), embeds.dtype)
-        for step_away in range(group_size):
-            hidden = lax.cond(jnp.any(distance == step_away), functools.partial(send_embeds, step_away), lambda same: same, hidden)
+            return lax.ppermute(rows, 'kv', shift_by(group_size, step_away)) if step_away else rows
+
+        def send_most(step_away, near_meta, clear_slot):
+            rows = send_embeds(step_away)
+            packed = pack_rows(tuple(range(layers)), k_pool, v_pool, near_meta, near_cap, [other_shape, far_shape, far_shape])
+            return rows, packed, copy_pools(k_pool, v_pool), pack_pages(tuple(range(layers)), k_pool, v_pool, clear_slot)
+
+        def send_rest(hidden):
+            for step_away in range(group_size):
+                hidden = lax.cond((counts[step_away] > 0) & (most != step_away), lambda rows, step_away=step_away: rows + send_embeds(step_away), lambda rows: rows, hidden)
+            return hidden
+
+        hidden, packed, (k_base, v_base), full_out = lax.switch(most, [functools.partial(send_most, step_away) for step_away in range(group_size)], gate(near_meta.astype(I32)), clear_slot)
+        *near_out, other, far_0, far_1 = packed
+        full_out = list(full_out)
+        hidden = lax.cond(all_same, lambda rows: rows, send_rest, hidden)
         hidden = hidden.reshape(per_dev * STEPS, width)
-        near_out[0], hidden = lax.optimization_barrier((near_out[0], hidden))
         near = [lax.ppermute(near_out[0], 'kv', shift_by(group_size, -1))]
 
         wanted = ~(is_local | in_moved | is_near)
         kind = jnp.where(is_local, LOCAL, jnp.where(in_moved, MOVED, jnp.where(is_near, NEXT, OTHER)))
         target = pos[:, None] * page_count + page_ids
         entry_dst = jnp.broadcast_to(dev[:, None], page_src.shape)
-        other = other_pages(k_pool, v_pool, other, page_src.reshape(-1), page_slot.reshape(-1), entry_dst.reshape(-1), target.reshape(-1), wanted.reshape(-1), me, group_size)
+
+        def fetch_other(buffer):
+            return other_pages(k_pool, v_pool, buffer, page_src.reshape(-1), page_slot.reshape(-1), entry_dst.reshape(-1), target.reshape(-1), wanted.reshape(-1), me, group_size)
+
+        other, moved[0] = lax.optimization_barrier((other, moved[0]))
+        other = lax.cond(jnp.any(wanted), fetch_other, lambda buffer: buffer, other)
         mine = place[None, :] == (me * per_dev + jnp.arange(per_dev, dtype=I32))[:, None]
         facts = []
         for layer in range(layers):
@@ -548,11 +574,6 @@
             prev_rows.append(lax.ppermute(rows, 'kv', shift_by(group_size, 1)))
             q_rows = queries.reshape(per_dev, STEPS, num_heads, head_dim)
             if layer == 0:
-                k_src, v_src, q_rows = lax.optimization_barrier((k_pool, v_pool, q_rows))
-                k_base, v_base = copy_pools(k_src, v_src)
-                q_rows, k_base, v_base = lax.optimization_barrier((q_rows, k_base, v_base))
-            if layer == 0:
-                full_out = list(pack_pages(tuple(range(layers)), k_pool, v_pool, clear_slot))
                 for after in range(layers - 1, -1, -1):
                     full_out[after], moved[-1] = lax.optimization_barrier((full_out[after], moved[-1]))
                     moved.append(lax.psum(full_out[after], 'kv'))
@@ -579,11 +600,14 @@
             sel = (at_pos & (my_distance == step_away)[None, :]).astype(hidden.dtype)
             return jnp.einsum('pb,ptd->tbd', sel, rows, preferred_element_type=jnp.float32).astype(hidden.dtype), k_out, v_out
 
-        counts = jnp.sum(distance[None, :] == jnp.arange(group_size, dtype=I32)[:, None], axis=1)
-        most = jnp.argmax(counts).astype(I32)
         y_out, k_out, v_out = lax.switch(most, [functools.partial(bring_most, step_away) for step_away in range(group_size)], k_base, v_base)
-        for step_away in range(group_size):
-            y_out = lax.cond((counts[step_away] > 0) & (most != step_away), functools.partial(bring_home, step_away), lambda same: same, y_out)
+
+        def bring_rest(y_out):
+            for step_away in range(group_size):
+                y_out = lax.cond((counts[step_away] > 0) & (most != step_away), functools.partial(bring_home, step_away), lambda same: same, y_out)
+            return y_out
+
+        y_out = lax.cond(all_same, lambda same: same, bring_rest, y_out)
         return y_out, k_out, v_out
 
     return jax.shard_map(device_fn, mesh=mesh, in_specs=(tok_spec, P(), P(), P(), P(), P(), P(), pool_spec, pool_spec, P('rep', None), P('rep'), P('rep'), P('rep')), out_specs=(tok_spec, pool_spec, pool_spec), check_vma=False)

time: 525 us -> 511 us (0.973)
  waiting for transfers between devices: 113 us -> 85 us
  between operations: 31 us -> 19.5 us
  matrix products: 180 us -> 191 us
  loops' own time: 1.38 us -> 8.24 us
    ppermute x2 -> x4, starting transfers between devices: 0.41 us -> 22.7 us  [pair_mlp(): rest = lax.ppermute(part[rows:], 'kv', pairs)]
    ppermute x2, starting transfers between devices: 22.9 us -> 1 us  [device_fn(): prev_rows.append(lax.ppermute(rows, 'kv', shift_by(group_size, 1)))]
    ppermute x1, waiting for transfers between devices: 15.1 us -> 0.01 us  [send_embeds(): lax.ppermute(rows, 'kv', shift_by(group_size, step_away))]
    dot_general x12 -> x14, matrix products: 178 us -> 189 us  [dense(): return jnp.dot(hidden, weight, preferred_element_type=jnp.float32)]
    psum x1, waiting for transfers between devices: 9.67 us -> 0.01 us  [device_fn(): moved = [lax.psum(moved_out, 'kv')]]
    another operation x17 -> x4, loops' own time: 1.09 us -> 7.98 us  [the longest x1 7.85 us: device_fn(): hidden = lax.cond(all_same, lambda rows: rows, send_rest, hidden)]
    psum x2, waiting for transfers between devices: 83.1 us -> 77.7 us  [device_fn(): moved.append(lax.psum(full_out[after], 'kv'))]
    unnamed x113 -> x114, local copies, waits for them, and re-layouts: 13.5 us -> 12.9 us
  transfers between devices with their start and end apart: 13 -> 15, of which waited for: 6 -> 6; matrix products, arithmetic and copies ran while one was open for 26% -> 41% of each run, Pallas kernels for 8% -> 10%
where the time goes in v2:
time: 511 us; the launch traced here: 501 us
  matrix products  191 us (37%)
  Pallas kernels  104 us (20%)
  waiting for transfers between devices  85 us (17%)
  local copies, waits for them, and re-layouts  31.8 us (6%)
  starting transfers between devices  30.6 us (6%)
  other arithmetic  30.6 us (6%)
  between operations  19.5 us (4%)
  loops' own time  8.24 us (2%)
    dot_general x14, matrix products, dense(): return jnp.dot(hidden, weight, preferred_element_type=jnp.float32)  189 us
    psum x2, waiting for transfers between devices, device_fn(): moved.append(lax.psum(full_out[after], 'kv'))  77.7 us
    pallas_call x2, Pallas kernels, attend(): pl.pallas_call(functools.partial(attend_kernel, layer, seqs, page_len, nu...  46.2 us
    ppermute x4, starting transfers between devices, pair_mlp(): rest = lax.ppermute(part[rows:], 'kv', pairs)  22.7 us
    pallas_call x1, Pallas kernels, copy_pools(): pl.pallas_call(copy_kernel, out_shape=[pool, pool], in_specs=[any_spec(),...  17.6 us
    pallas_call x1, Pallas kernels, finish_pools(): pl.pallas_call(functools.partial(finish_kernel, layers, slots, entries),...  17.4 us
    pallas_call x2, Pallas kernels, pack_rows(): pl.pallas_call(functools.partial(pack_rows_kernel, layers), out_shape=out...  15.3 us
    unnamed x114, local copies, waits for them, and re-layouts  12.9 us
  transfers between devices with their start and end apart: 15, of which 6 were waited for; matrix products, arithmetic and copies ran while one was open for 41% of the time, Pallas kernels for 10%

profile of v2, /device:TPU:0, one launch (start us, length us, event | category | flops | bytes accessed | tf_op | source)
XLA Modules:
  0.0 501.2 jit_solution(4386927015671390190)
XLA Ops:
  13.9 6.2 %shard_map.166 = bf16[2,672,8,128]{3,2,1,0:T(8,128)(2,1)} custom-call(s32[3,64]{1,0:T(4,128)} %pad_add_fusion.3.meta, bf16[192,2,16,8,128]{4,3,2,1,0:T(8,128)(2,1)} %k_pool.5, bf16[192,2,16,8,128]{4,3,2,1,0:T(8,128)(2,1)} %v_pool.5), custom_call_target="tpu_custom_call" | custom-call | flops 10000000000 | bytes 10000000 | tf_op jit(solution)/shard_map/pallas_call | solution.py:165
  28.0 35.1 %conditional.44 = (bf16[64,2,4096]{2,0,1:T(8,128)(2,1)}, bf16[2,608,8,128]{3,2,1,0:T(8,128)(2,1)}, bf16[2,608,8,128]{3,2,1,0:T(8,128)(2,1)}, bf16[128,2,2,16,8,1...) conditional(s32[]{:T(128)} %clamp.4, (s32[64]{0:T(128)}, ...), branch_computations={%region_15.16_spmd, %region_16.17_spmd, %region_17.18_spmd, %regio... | conditional | flops 30067638272 | bytes 36304248 | solution.py:536
  29.3 17.6 %copy_pools.9 = (bf16[192,2,16,8,128]{4,3,2,1,0:T(8,128)(2,1)}, bf16[192,2,16,8,128]{4,3,2,1,0:T(8,128)(2,1)}) custom-call(bf16[192,2,16,8,128]{4,3,2,1,0:T(8,128)(2,1)} %get-tuple-element.762.k_pool, bf16[192,2,16,8,128]{4,3,2,1,0:T(8,128)(2,1)} %get-tuple-element.763.v_pool), custom_call_target="tpu_custom_call" | custom-call | flops 10000000000 | bytes 10000000 | tf_op jit(solution)/shard_map/cond/branch_1_fun/copy_pools/pallas_call | solution.py:303
  46.9 7.0 %branch_1_fun.3 = (bf16[2,1024,8,128]{3,2,1,0:T(8,128)(2,1)}, bf16[2,1024,8,128]{3,2,1,0:T(8,128)(2,1)}) custom-call(s32[1,64]{1,0:T(1,128)S(1)} %bitcast.436, bf16[192,2,16,8,128]{4,3,2,1,0:T(8,128)(2,1)} %get-tuple-element.762.k_pool, bf16[192,2,16,8,128]{4,3,2,1,0:T(8,128)(2,1)} %get-tuple-element.763.v_pool), custom_call_target="tpu_custom_call" | custom-call | flops 10000000000 | bytes 10000000 | tf_op jit(solution)/shard_map/cond/branch_1_fun/pallas_call | solution.py:112
  54.0 9.2 %branch_1_fun.2 = (bf16[2,608,8,128]{3,2,1,0:T(8,128)(2,1)}, bf16[2,608,8,128]{3,2,1,0:T(8,128)(2,1)}, bf16[128,2,2,16,8,128]{5,4,3,2,1,0:T(8,128)(2,1)}, bf16[5...) custom-call(s32[3,64]{1,0:T(4,128)S(1)} %get-tuple-element.761.meta, ...), custom_call_target="tpu_custom_call" | custom-call | flops 10000000000 | bytes 10000000 | tf_op jit(solution)/shard_map/cond/branch_1_fun/pallas_call | solution.py:165
  70.9 16.4 %conditional.45 = (bf16[128,4096]{1,0:T(8,128)(2,1)}, bf16[128,4096]{1,0:T(8,128)(2,1)}, f32[128,4096]{1,0:T(8,128)}) conditional(s32[]{:T(128)} %bitcast.80, (s32[8]{0:T(128)S(1)}, s32[]{:T(128)}, bf16[64,2,4096]{2,0,1:T(8,128)(2,1)}, s32[64]{0:T(128)}, pred[64,64]{0,1:T(32,128)(4,1)S(1)}, ...), branch_computations={%region_23.40_spmd, %region_40.41_spmd} | conditional | flops 545817088 | bytes 78688280 | solution.py:539
  93.0 13.2 %fusion.222 = bf16[16,8,32,128]{3,1,2,0:T(8,128)(2,1)S(1)} fusion(bf16[128,4096]{1,0:T(8,128)(2,1)} %get-tuple-element.1184, bf16[2,4096,4096]{2,1,0:T(8,128)(2,1)} %param.76), kind=kOutput, calls=%fused_computation.289 | convolution fusion | flops 4295491584 | bytes 35651584 | tf_op jit(solution)/shard_map/dot_general | solution.py:412
  107.7 5.7 %fusion.246 = bf16[16,8,8,128]{3,1,2,0:T(8,128)(2,1)} fusion(bf16[128,4096]{1,0:T(8,128)(2,1)} %get-tuple-element.1184, bf16[2,4096,1024]{2,1,0:T(8,128)(2,1)} %param.77), kind=kOutput, calls=%fused_computation.301 | convolution fusion | flops 1073872896 | bytes 9699328 | tf_op jit(solution)/shard_map/dot_general | solution.py:412
  127.4 23.0 %shard_map.167 = bf16[64,2,32,128]{3,2,1,0:T(8,128)(2,1)} custom-call(s32[5,64]{1,0:T(8,128)} %get-tuple-element.2224.meta, bf16[64,2,32,128]{3,2,1,0:T(8,128)(2,1)} %bitcast.401, bf16[64,2,2,8,128]{4,3,2,1,0:T(8,128)(2,1)} %maximum_bitcast_fusion.new_ref, bf16[192,2,16,8,128]{4,3,2,1,0:T(8,128)(2,1)} %k_pool.5, bf16[192,2,16,8,128]{4,3,2,1,0:T(8,128)(2,1)} %v_pool.5, ...), custom_call_target="tpu_custom_call" | custom-call | flops 10000000000 | bytes 10000000 | tf_op jit(solution)/shard_map/pallas_call | solution.py:270
  150.4 14.0 %fusion.204 = bf16[128,4096]{1,0:T(8,128)(2,1)S(1)} fusion(f32[128,4096]{1,0:T(8,128)} %get-tuple-element.2152, bf16[2,4096,4096]{2,1,0:T(8,128)(2,1)} %param.79, bf16[16,8,32,128]{3,2,1,0:T(8,128)(2,1)} %bitcast.403), kind=kOutput, calls=%fused_computation.279 | convolution fusion | flops 4296015872 | bytes 37748736 | tf_op jit(solution)/shard_map/dot_general | solution.py:412
  167.1 28.0 %fusion.182 = bf16[256,7168]{1,0:T(8,128)(2,1)} fusion(bf16[2,4096,14336]{2,1,0:T(8,128)(2,1)} %param.80, s32[]{:T(128)S(6)} %select_n.392, bf16[128,4096]{1,0:T(8,128)(2,1)S(1)} %collective-permute-done.29, bf16[128,4096]{1,0:T(8,128)(2,1)S(1)} %fusion.204), kind=kOutput, calls=%fused_computation.269 | convolution fusion | flops 15056764928 | bytes 64487428 | tf_op jit(solution)/shard_map/dot_general | solution.py:412
  195.1 15.0 %fusion.151 = f32[256,2048]{1,0:T(8,128)S(1)} fusion(bf16[256,7168]{1,0:T(8,128)(2,1)} %fusion.182, bf16[2,14336,4096]{2,1,0:T(8,128)(2,1)} %param.81, s32[]{:T(128)S(6)} %select_n.392), kind=kOutput, calls=%fused_computation.236 | convolution fusion | flops 7516192768 | bytes 35127300 | tf_op jit(solution)/shard_map/dot_general | solution.py:412
  210.2 16.7 %fusion.149 = f32[256,2048]{1,0:T(8,128)S(1)} fusion(bf16[256,7168]{1,0:T(8,128)(2,1)} %fusion.182, bf16[2,14336,4096]{2,1,0:T(8,128)(2,1)} %param.81, s32[]{:T(128)S(6)} %select_n.392), kind=kOutput, calls=%fused_computation.234 | convolution fusion | flops 7516192768 | bytes 35127300 | tf_op jit(solution)/shard_map/dot_general | solution.py:412
  231.1 5.9 %all-reduce.6.cloned.1.call-done.moved = bf16[2,1024,8,128]{3,2,1,0:T(8,128)(2,1)} async-done(((bf16[2,1024,8,128]{3,2,1,0:T(8,128)(2,1)}), bf16[2,1024,8,128]{3,2,1,0:T(8,128)(2,1)}) %all-reduce.6.cloned.1.call-update) | async-done | bytes 4194320 | tf_op jit(solution)/shard_map/psum | solution.py:579
  251.4 13.2 %fusion.219 = bf16[16,8,32,128]{3,1,2,0:T(8,128)(2,1)S(1)} fusion(bf16[2,4096,4096]{2,1,0:T(8,128)(2,1)} %param.76, bf16[128,2048]{1,0:T(8,128)(2,1)} %copy-done.15, bf16[128,2048]{1,0:T(8,128)(2,1)} %copy-done.13), kind=kOutput, calls=%fused_computation.288 | convolution fusion | flops 4297588736 | bytes 35651584 | tf_op jit(solution)/shard_map/dot_general | solution.py:412
  269.2 23.2 %shard_map.168 = bf16[64,2,32,128]{3,2,1,0:T(8,128)(2,1)} custom-call(s32[5,64]{1,0:T(8,128)} %get-tuple-element.2225.meta, bf16[64,2,32,128]{3,2,1,0:T(8,128)(2,1)} %bitcast.402, bf16[64,2,2,8,128]{4,3,2,1,0:T(8,128)(2,1)} %maximum_bitcast_fusion.1.new_ref, bf16[192,2,16,8,128]{4,3,2,1,0:T(8,128)(2,1)} %k_pool.5, bf16[192,2,16,8,128]{4,3,2,1,0:T(8,128)(2,1)} %v_pool.5, ...), custom_call_target="tpu_custom_call" | custom-call | flops 10000000000 | bytes 10000000 | tf_op jit(solution)/shard_map/pallas_call | solution.py:270
  292.5 13.7 %fusion.201 = bf16[128,4096]{1,0:T(8,128)(2,1)S(1)} fusion(bf16[2,4096,4096]{2,1,0:T(8,128)(2,1)} %param.79, bf16[16,8,32,128]{3,2,1,0:T(8,128)(2,1)} %bitcast.404, bf16[128,2048]{1,0:T(8,128)(2,1)S(1)} %copy-done.16, bf16[128,2048]{1,0:T(8,128)(2,1)S(1)} %copy-done.14), kind=kOutput, calls=%fused_computation.278 | convolution fusion | flops 4298113024 | bytes 36700160 | tf_op jit(solution)/shard_map/dot_general | solution.py:412
  309.0 25.2 %fusion.192 = bf16[256,7168]{1,0:T(8,128)(2,1)} fusion(bf16[2,4096,14336]{2,1,0:T(8,128)(2,1)} %param.80, s32[]{:T(128)S(6)} %select_n.392, bf16[128,4096]{1,0:T(8,128)(2,1)} %collective-permute-done.33, bf16[128,4096]{1,0:T(8,128)(2,1)S(1)} %fusion.201), kind=kOutput, calls=%fused_computation.275 | convolution fusion | flops 15056764928 | bytes 64487428 | tf_op jit(solution)/shard_map/dot_general | solution.py:412
  334.2 14.4 %fusion.145 = f32[256,2048]{1,0:T(8,128)S(1)} fusion(bf16[256,7168]{1,0:T(8,128)(2,1)} %fusion.192, bf16[2,14336,4096]{2,1,0:T(8,128)(2,1)} %param.81, s32[]{:T(128)S(6)} %select_n.392), kind=kOutput, calls=%fused_computation.230 | convolution fusion | flops 7516192768 | bytes 35127300 | tf_op jit(solution)/shard_map/dot_general | solution.py:412
  348.6 14.7 %fusion.147 = f32[256,2048]{1,0:T(8,128)S(1)} fusion(bf16[256,7168]{1,0:T(8,128)(2,1)} %fusion.192, bf16[2,14336,4096]{2,1,0:T(8,128)(2,1)} %param.81, s32[]{:T(128)S(6)} %select_n.392), kind=kOutput, calls=%fused_computation.232 | convolution fusion | flops 7516192768 | bytes 35127300 | tf_op jit(solution)/shard_map/dot_general | solution.py:412
  366.8 22.3 %collective-permute-start.35 = (f32[128,2048]{1,0:T(8,128)}, f32[128,2048]{1,0:T(8,128)}, u32[]{:S(2)}, u32[]{:S(2)}) collective-permute-start(f32[128,2048]{1,0:T(8,128)} %slice.214), channel_id=1, source_target_pairs={{0,1},{1,0},{2,3},{3,2},{4,5},{5,4},{6,7},{7,6}} | collective-permute-start | bytes 3145736 | tf_op jit(solution)/shard_map/ppermute | solution.py:425
  396.0 71.8 %all-reduce.8.cloned.1.call-done = bf16[2,1024,8,128]{3,2,1,0:T(8,128)(2,1)} async-done(((bf16[2,1024,8,128]{3,2,1,0:T(8,128)(2,1)}), bf16[2,1024,8,128]{3,2,1,0:T(8,128)(2,1)}) %all-reduce.8.cloned.1.call-update) | async-done | bytes 4194320 | tf_op jit(solution)/shard_map/psum | solution.py:579
  468.6 23.5 %conditional.48 = (bf16[192,2,16,8,128]{4,3,2,1,0:T(8,128)(2,1)}, bf16[192,2,16,8,128]{4,3,2,1,0:T(8,128)(2,1)}, bf16[2,64,4096]{2,1,0:T(8,128)(2,1)}, bf16[2,64,4096]{2,1,0:T(8,128)(2,1)S(1)}) conditional(s32[]{:T(128)} %clamp.4, (s32[2,64]{1,0:T(2,128)S(1)}, s32[3,192]{1,0:T(4,128)S(1)}, ...), branch_computations={%region_62.64_spmd, %region_63.65_spmd, %region_64.66_spmd, %regio... | conditional | flops 10067637248 | bytes 20490312
  471.7 17.4 %finish_pools.9 = (bf16[192,2,16,8,128]{4,3,2,1,0:T(8,128)(2,1)}, bf16[192,2,16,8,128]{4,3,2,1,0:T(8,128)(2,1)}) custom-call(s32[2,64]{1,0:T(2,128)S(1)} %get-tuple-element.952.mig, s32[3,192]{1,0:T(4,128)S(1)} %get-tuple-element.953.owner, bf16[192,2,16,8,128]{4,3,2,1,0:T(8,128)(2,1)} %get-tuple-element.954.k_in, ...), custom_call_target="tpu_custom_call", output_to_operand_aliasing={{0}: (2, {}), {1}: (3, {})} | custom-call | flops 10000000000 | bytes 10000000 | tf_op jit(solution)/shard_map/cond/branch_1_fun/finish_pools/pallas_call | solution.py:388
  (235 shorter events, 97.3 us)
Async XLA Ops:
  7.2 118.5 %all-reduce.4.cloned.1.call-start = ((), (), s32[]{:S(2)}) async-start(), calls=%async_computation.2 | async-start | bytes 5505024 | tf_op jit(solution)/shard_map/psum | solution.py:490
  25.8 45.1 %copy-start.2 = (pred[64,64]{0,1:T(32,128)(4,1)}, pred[64,64]{0,1:T(32,128)(4,1)S(1)}, u32[]{:S(2)}) copy-start(pred[64,64]{0,1:T(32,128)(4,1)S(1)} %iota_compare_fusion.2) | copy-start | bytes 12292
  28.0 39.7 %copy-start.23 = (s32[512,2]{0,1:T(2,128)S(1)}, s32[512,2]{0,1:T(2,128)}, u32[]{:S(2)}) copy-start(s32[512,2]{0,1:T(2,128)} %copy-done.22) | copy-start | bytes 12292
  28.0 41.6 %copy-start.18 = (s32[8]{0:T(128)S(1)}, s32[8]{0:T(128)}, u32[]{:S(2)}) copy-start(s32[8]{0:T(128)} %copy-done.17) | copy-start | bytes 100
  29.3 33.9 %collective-permute-start = (bf16[64,2,4096]{2,0,1:T(8,128)(2,1)S(1)}, bf16[64,2,4096]{2,0,1:T(8,128)(2,1)}, u32[]{:S(2)}, u32[]{:S(2)}) collective-permute-start(bf16[64,2,4096]{2,0,1:T(8,128)(2,1)S(1)} %convolution_convert_fusion.1), channel_id=1, source_target_pairs={{0,1},{1,2},{2,3},{3,4},{4,5},{5,6},{6,7},{7,0}} | collective-permute-start | bytes 3145736 | tf_op jit(solution)/shard_map/cond/branch_1_fun/ppermute | solution.py:524
  63.2 62.8 %collective-permute-start.28 = (bf16[2,608,8,128]{3,2,1,0:T(8,128)(2,1)}, bf16[2,608,8,128]{3,2,1,0:T(8,128)(2,1)S(1)}, u32[]{:S(2)}, u32[]{:S(2)}) collective-permute-start(bf16[2,608,8,128]{3,2,1,0:T(8,128)(2,1)} %get-tuple-element.1162), channel_id=1, source_target_pairs={{0,7},{1,0},{2,1},{3,2},{4,3},{5,4},{6,5},{7,6}} | collective-permute-start | bytes 7471112 | tf_op jit(solution)/shard_map/ppermute | solution.py:541
  125.7 111.3 %all-reduce.6.cloned.1.call-start = ((), (), s32[]{:S(2)}) async-start(), calls=%async_computation.3 | async-start | bytes 8388608 | tf_op jit(solution)/shard_map/psum | solution.py:579
  164.4 30.7 %copy-start.12 = (bf16[128,4096]{1,0:T(8,128)(2,1)}, bf16[128,4096]{1,0:T(8,128)(2,1)S(1)}, u32[]{:S(2)}) copy-start(bf16[128,4096]{1,0:T(8,128)(2,1)S(1)} %fusion.204) | copy-start | bytes 3145732
  164.4 2.7 collective-permute-start.29
  164.5 303.3 %all-reduce.8.cloned.1.call-start = ((), (), s32[]{:S(2)}) async-start(), calls=%async_computation.4 | async-start | bytes 8388608 | tf_op jit(solution)/shard_map/psum | solution.py:579
  228.0 9.0 %collective-permute-start.31 = (f32[128,2048]{1,0:T(8,128)}, f32[128,2048]{1,0:T(8,128)}, u32[]{:S(2)}, u32[]{:S(2)}) collective-permute-start(f32[128,2048]{1,0:T(8,128)} %slice.207), channel_id=1, source_target_pairs={{0,1},{1,0},{2,3},{3,2},{4,5},{5,4},{6,7},{7,6}} | collective-permute-start | bytes 3145736 | tf_op jit(solution)/shard_map/ppermute | solution.py:425
  228.6 8.5 %collective-permute-start.30 = (f32[128,2048]{1,0:T(8,128)S(1)}, f32[128,2048]{1,0:T(8,128)}, u32[]{:S(2)}, u32[]{:S(2)}) collective-permute-start(f32[128,2048]{1,0:T(8,128)S(1)} %slice.204), channel_id=1, source_target_pairs={{0,1},{1,0},{2,3},{3,2},{4,5},{5,4},{6,7},{7,6}} | collective-permute-start | bytes 3145736 | tf_op jit(solution)/shard_map/ppermute | solution.py:425
  228.8 39.0 %collective-permute-start.32 = (bf16[2,608,8,128]{3,2,1,0:T(8,128)(2,1)}, bf16[2,608,8,128]{3,2,1,0:T(8,128)(2,1)S(1)}, u32[]{:S(2)}, u32[]{:S(2)}) collective-permute-start(bf16[2,608,8,128]{3,2,1,0:T(8,128)(2,1)} %get-tuple-element.1168), channel_id=1, source_target_pairs={{0,7},{1,0},{2,1},{3,2},{4,3},{5,4},{6,5},{7,6}} | collective-permute-start | bytes 7471112 | tf_op jit(solution)/shard_map/ppermute | solution.py:583
  306.2 2.8 collective-permute-start.33
  306.3 162.3 %collective-permute-start.36 = (bf16[64,2,2,8,128]{4,3,2,1,0:T(8,128)(2,1)}, bf16[64,2,2,8,128]{4,3,2,1,0:T(8,128)(2,1)S(1)}, u32[]{:S(2)}, u32[]{:S(2)}) collective-permute-start(bf16[64,2,2,8,128]{4,3,2,1,0:T(8,128)(2,1)} %maximum_bitcast_fusion.new_ref), channel_id=1, source_target_pairs={{0,1},{1,2},{2,3},{3,4},{4,5},{5,6},{6,7},{7,0}} | collective-permute-start | bytes 1572872 | tf_op jit(solution)/shard_map/ppermute | solution.py:574
  364.7 25.0 %copy-start.56 = (s32[64]{0:T(128)S(1)}, s32[64]{0:T(128)}, u32[]{:S(2)}) copy-start(s32[64]{0:T(128)} %copy-done.55) | copy-start | bytes 772
  364.7 25.1 %copy-start.42 = (s32[512]{0:T(512)S(1)}, s32[512]{0:T(512)}, u32[]{:S(2)}) copy-start(s32[512]{0:T(512)} %copy-done.41) | copy-start | bytes 6148
  364.7 25.1 %copy-start.45 = (s32[512,1]{0,1:T(1,128)S(1)}, s32[512,1]{0,1:T(1,128)}, u32[]{:S(2)}) copy-start(s32[512,1]{0,1:T(1,128)} %copy-done.44) | copy-start | bytes 6148
  364.7 25.5 %copy-start.57 = (s32[3]{0:T(128)S(1)}, s32[3]{0:T(128)}, u32[]{:S(2)}) copy-start(s32[3]{0:T(128)} %constant.333) | copy-start | bytes 40
  366.8 25.0 %collective-permute-start.35 = (f32[128,2048]{1,0:T(8,128)}, f32[128,2048]{1,0:T(8,128)}, u32[]{:S(2)}, u32[]{:S(2)}) collective-permute-start(f32[128,2048]{1,0:T(8,128)} %slice.214), channel_id=1, source_target_pairs={{0,1},{1,0},{2,3},{3,2},{4,5},{5,4},{6,7},{7,6}} | collective-permute-start | bytes 3145736 | tf_op jit(solution)/shard_map/ppermute | solution.py:425
  389.1 4.1 collective-permute-start.34
  390.3 78.3 %collective-permute-start.37 = (bf16[64,2,2,8,128]{4,3,2,1,0:T(8,128)(2,1)}, bf16[64,2,2,8,128]{4,3,2,1,0:T(8,128)(2,1)S(1)}, u32[]{:S(2)}, u32[]{:S(2)}) collective-permute-start(bf16[64,2,2,8,128]{4,3,2,1,0:T(8,128)(2,1)} %maximum_bitcast_fusion.1.new_ref), channel_id=1, source_target_pairs={{0,1},{1,2},{2,3},{3,4},{4,5},{5,6},{6,7},{7,0}} | collective-permute-start | bytes 1572872 | tf_op jit(solution)/shard_map/ppermute | solution.py:574
  395.9 72.6 %copy-start.3 = (pred[64,64]{0,1:T(32,128)(4,1)S(1)}, pred[64,64]{0,1:T(32,128)(4,1)}, u32[]{:S(2)}) copy-start(pred[64,64]{0,1:T(32,128)(4,1)} %copy-done.2) | copy-start | bytes 12292
  470.2 19.0 %collective-permute-start.14 = (bf16[64,2,4096]{2,0,1:T(8,128)(2,1)}, bf16[64,2,4096]{2,0,1:T(8,128)(2,1)S(1)}, u32[]{:S(2)}, u32[]{:S(2)}) collective-permute-start(bf16[64,2,4096]{2,0,1:T(8,128)(2,1)} %copy.150), channel_id=1, source_target_pairs={{0,7},{1,0},{2,1},{3,2},{4,3},{5,4},{6,5},{7,6}} | collective-permute-start | bytes 3145736 | tf_op jit(solution)/shard_map/cond/branch_1_fun/ppermute | solution.py:598
  (45 other events, 411.3 us)
Sparse Core Ops, SparseCore 0:
  20.2 65.2 all-reduce.3
  164.6 72.3 all-reduce.5
  389.9 77.9 all-reduce.7
